TPU v7x, 32 devices: a whole 2x2x4 slice. The times are simulated.
32 devices in a mesh: groups: 2 (over y), gx: 16 (over z, x, core).
Axes of the slice: x: 2, y: 2, z: 4, core: 2. Of those that a mesh axis runs over, the one named last changes fastest.
Arguments:
- stream_in: bfloat16 [32, 8192], P(('groups', 'gx')), parts along dimension 0, may hold values from -6 to 6
- query: bfloat16 [32, 8192], P(('groups', 'gx')), parts along dimension 0, may hold values from -4.5 to 4.5
- key_new: bfloat16 [32, 1024], P(('groups', 'gx')), parts along dimension 0, may hold values from -4.5 to 4.5
- value_new: bfloat16 [32, 1024], P(('groups', 'gx')), parts along dimension 0, may hold values from -6 to 6
- key_cache: bfloat16 [32, 128, 1024], P(('groups', 'gx')), parts along dimension 0, may hold values from -6 to 6
- value_cache: bfloat16 [32, 128, 1024], P(('groups', 'gx')), parts along dimension 0, may hold values from -6 to 6
- lengths: int32 [32], P(('groups', 'gx')), parts along dimension 0, may hold values from 1 to 128, as said below
- route_ids: int32 [32, 2], P(('groups', 'gx')), parts along dimension 0, may hold values from 0 to 3, as said below
- route_scores: float32 [32, 2], P(('groups', 'gx')), parts along dimension 0, may hold values from -6 to 6
- out_weight: bfloat16 [8192, 8192], P(None, 'gx'), may hold values from -0.0625 to 0.0625
- norm_gain: float32 [8192], replicated, may hold values from 0.1 to 1.9
- gate_weight: bfloat16 [2, 16384, 7168], P(None, 'gx'), may hold values from -0.0625 to 0.0625
- up_weight: bfloat16 [2, 16384, 7168], P(None, 'gx'), may hold values from -0.0625 to 0.0625
- down_weight: bfloat16 [2, 114688, 1024], P(None, 'gx'), may hold values from -0.046875 to 0.046875
Outputs:
- layer_out: bfloat16 [32, 8192], P(('groups', 'gx')), parts along dimension 0
There are 2 independent parts, one for each index of `groups`. A program takes and returns all parts, laid end to end along the dimension named above; an argument that names none is the same for every part. Nothing has to cross between parts.
Inputs may be any that keep to these rules, and one draw needn't show every extreme that they name: `lengths`: 1 to 128; some sequence fills all 128 slots. `route_ids`: each row names two different experts of 0 to 3; in one replica's batch each of the experts 0 and 1 is named by at most 10 sequences, and one of them by exactly 10.
All inputs are finite; a program needn't handle non-finite values.
Results may differ from a plain program's by a relative error of at most 0.0095.
Values may be sent and summed in bfloat16 or wider, within the bound.
No kernel may reach another device: no remote copies, remote signals or barrier semaphores. Data moves between devices by JAX's collectives and lax.ppermute only.
A program may use at most 192 MiB of HBM per device.

v0:
```python
import jax
import jax.numpy as jnp
from jax import lax
from jax.sharding import PartitionSpec as P

NH = 64
KVH = 8
HS = 128
RESIDENT = 2
MSPLIT = 8


def partner(value, axis, distance):
    return lax.ppermute(value, axis, [(i, i ^ 1 << distance) for i in range(lax.axis_size(axis))])


def attend_local(query, key_new, value_new, key_cache, value_cache, lengths):
    seqs = query.shape[0]
    slots = key_cache.shape[1]
    group = NH // KVH
    scale = HS ** (-0.5)
    q_four = query.reshape(seqs, KVH, group, HS)
    k_all = key_cache.reshape(seqs, slots, KVH, HS)
    v_all = value_cache.reshape(seqs, slots, KVH, HS)
    k_own = key_new.reshape(seqs, KVH, HS)
    v_own = value_new.reshape(seqs, KVH, HS)
    scores = (
        jnp.einsum("skgd,sckd->skgc", q_four, k_all, preferred_element_type=jnp.float32) * scale
    )
    live = jnp.arange(slots, dtype=jnp.int32)[None, :] < lengths[:, None]
    scores = jnp.where(live[:, None, None, :], scores, -1e30)
    own = jnp.einsum("skgd,skd->skg", q_four, k_own, preferred_element_type=jnp.float32) * scale
    top = jnp.maximum(jnp.max(scores, axis=-1), own)
    e_cache = jnp.exp(scores - top[..., None])
    e_own = jnp.exp(own - top)
    total = jnp.sum(e_cache, axis=-1) + e_own
    p_cache = (e_cache / total[..., None]).astype(jnp.bfloat16)
    p_own = (e_own / total).astype(jnp.bfloat16)
    mixed = jnp.einsum("skgc,sckd->skgd", p_cache, v_all, preferred_element_type=jnp.float32)
    mixed = mixed + p_own.astype(jnp.float32)[..., None] * v_own.astype(jnp.float32)[:, :, None, :]
    return mixed.reshape(seqs, NH * HS).astype(jnp.bfloat16)


def gated(parts):
    return (jax.nn.silu(parts[..., 0, :]) * parts[..., 1, :]).astype(jnp.bfloat16)


def on_device(
    stream_in,
    query,
    key_new,
    value_new,
    key_cache,
    value_cache,
    lengths,
    route_ids,
    route_scores,
    out_weight,
    norm_gain,
    gate_weight,
    up_weight,
    down_weight,
):
    seqs = stream_in.shape[0]
    width = stream_in.shape[1]
    members = lax.axis_size("gx")
    batch = seqs * members
    hsplit = members // MSPLIT
    low_bits = hsplit.bit_length() - 1
    model_bits = MSPLIT.bit_length() - 1
    place = lax.axis_index("gx")
    model_block = place // hsplit
    block_width = width // MSPLIT
    hidden_cols = gate_weight.shape[2]
    narrow = hidden_cols // MSPLIT
    attn = attend_local(query, key_new, value_new, key_cache, value_cache, lengths)
    proj_cols = jnp.dot(
        lax.all_gather(attn, "gx", axis=0, tiled=True),
        out_weight,
        preferred_element_type=jnp.float32,
    ).astype(jnp.bfloat16)
    proj = lax.all_to_all(proj_cols, "gx", split_axis=0, concat_axis=1, tiled=True)
    resid = stream_in.astype(jnp.float32) + proj.astype(jnp.float32)
    power = jnp.mean(resid * resid, axis=-1, keepdims=True)
    normed = (resid * lax.rsqrt(power + 1e-05) * norm_gain).astype(jnp.bfloat16)
    probs = jax.nn.softmax(route_scores, axis=-1)
    columns = []
    for expert in range(RESIDENT):
        columns.append(jnp.sum(jnp.where(route_ids == expert, probs, 0.0), axis=-1))
    weight = jnp.stack(columns, axis=-1).astype(jnp.bfloat16)
    normed_all, weight_all = (
        lax.all_gather(normed, "gx", axis=0, tiled=True),
        lax.all_gather(weight, "gx", axis=0, tiled=True),
    )
    rows_in = lax.dynamic_slice_in_dim(normed_all, model_block * block_width, block_width, 1)
    gate_view = gate_weight.reshape(RESIDENT, block_width, MSPLIT, narrow)
    up_view = up_weight.reshape(RESIDENT, block_width, MSPLIT, narrow)
    gate_part = jnp.einsum("bd,rdpc->bprc", rows_in, gate_view, preferred_element_type=jnp.float32)
    up_part = jnp.einsum("bd,rdpc->bprc", rows_in, up_view, preferred_element_type=jnp.float32)
    parts = jnp.stack([gate_part, up_part], axis=3)
    for bit in range(model_bits):
        parts = parts + partner(parts.astype(jnp.bfloat16), "gx", low_bits + bit).astype(
            parts.dtype
        )
    hidden = gated(parts)
    down_view = down_weight.reshape(RESIDENT, MSPLIT, narrow, block_width)
    scales = weight_all.astype(jnp.float32)
    result = jnp.zeros((batch, block_width), jnp.float32)
    for expert in range(RESIDENT):
        term = jnp.einsum(
            "bpc,pcn->bn",
            hidden[:, :, expert],
            down_view[expert],
            preferred_element_type=jnp.float32,
        )
        result = result + scales[:, expert][:, None] * term
    partial_out = result.reshape(members, seqs, block_width)
    got = lax.all_to_all(
        partial_out.astype(jnp.bfloat16), "gx", split_axis=0, concat_axis=0, tiled=True
    ).astype(partial_out.dtype)
    got = jnp.sum(got.reshape(MSPLIT, hsplit, seqs, block_width), axis=1)
    ffn = got.transpose(1, 0, 2).reshape(seqs, width)
    return (resid + ffn).astype(jnp.bfloat16)


def solution(mesh):
    return jax.shard_map(
        on_device,
        mesh=mesh,
        in_specs=(
            P(("groups", "gx"), None),
            P(("groups", "gx"), None),
            P(("groups", "gx"), None),
            P(("groups", "gx"), None),
            P(("groups", "gx"), None, None),
            P(("groups", "gx"), None, None),
            P(("groups", "gx")),
            P(("groups", "gx"), None),
            P(("groups", "gx"), None),
            P(None, "gx"),
            P(),
            P(None, "gx", None),
            P(None, "gx", None),
            P(None, "gx", None),
        ),
        out_specs=P(("groups", "gx"), None),
        check_vma=False,
    )
```

profile of v0, /device:TPU:0, one launch (start us, length us, event | category | flops | bytes accessed | tf_op | source)
XLA Modules:
  0.0 213.6 jit_solution(13824069734522888616)
XLA Ops:
  0.7 0.7 convert_element_type.127
  1.4 1.0 copy.57
  2.4 0.1 reduce.10
  2.5 0.8 fusion.30
  3.3 0.3 fusion.42
  3.6 0.2 fusion.29
  3.8 1.0 copy.58
  4.8 0.2 fusion.20
  5.1 24.6 %all-gather = bf16[16,1,8192]{2,1,0:T(2,128)(2,1)S(1)} all-gather(bf16[1,1,8192]{2,1,0:T(2,128)(2,1)S(1)} %reshape.215), channel_id=1, replica_groups=mesh['groups'=2,'gx'=16] {'gx'}, dimensions={0}, use_global_device_ids=true | all-gather | bytes 278528 | tf_op jit(solution)/shard_map/all_gather | solution.py:78
  29.7 4.6 %fusion.21 = bf16[16,1,512]{2,0,1:T(8,128)(2,1)S(1)} fusion(bf16[8192,512]{1,0:T(8,128)(2,1)} %param.23, bf16[16,1,8192]{2,1,0:T(2,128)(2,1)S(1)} %all-gather), kind=kOutput, calls=%fused_computation.26 | convolution fusion | flops 134225920 | bytes 8667136 | tf_op jit(solution)/shard_map/dot_general | solution.py:77
  34.3 0.5 broadcast.44
  34.8 0.6 reduce.13
  35.4 0.6 reshape.233
  36.0 3.5 %all-to-all-start = ((bf16[16,2,256]{2,1,0:T(2,128)(2,1)}), bf16[16,2,256]{2,1,0:T(2,128)(2,1)S(1)}, u32[]{:S(2)}, u32[]{:S(2)}) async-start(bf16[16,2,256]{2,1,0:T(2,128)(2,1)} %reshape.233), calls=%async_computation | async-start | bytes 32768 | tf_op jit(solution)/shard_map/all_to_all | solution.py:82
  39.6 6.4 %all-to-all-done = bf16[16,2,256]{2,1,0:T(2,128)(2,1)S(1)} async-done(((bf16[16,2,256]{2,1,0:T(2,128)(2,1)}), bf16[16,2,256]{2,1,0:T(2,128)(2,1)S(1)}, u32[]{:S(2)}, u32[]{:S(2)}) %all-to-all-start) | async-done | bytes 16416 | tf_op jit(solution)/shard_map/all_to_all | solution.py:82
  46.0 0.7 multiply_reduce_fusion
  47.4 0.1 convert_bitcast_fusion
  47.5 19.1 %all-gather.2 = bf16[16,1,8192]{2,1,0:T(2,128)(2,1)S(1)} all-gather(bf16[1,1,8192]{2,1,0:T(2,128)(2,1)S(1)} %convert_bitcast_fusion), channel_id=1, replica_groups=mesh['groups'=2,'gx'=16] {'gx'}, dimensions={0}, use_global_device_ids=true | all-gather | bytes 278528 | tf_op jit(solution)/shard_map/all_gather | solution.py:92
  66.6 0.1 constant_dynamic-slice_fusion
  66.6 11.4 %fusion.10 = f32[16,8,2,1,896]{4,0,1,2,3:T(8,128)S(1)} fusion(bf16[2,128,8,8,896]{4,3,2,1,0:T(8,128)(2,1)} %bitcast.112, bf16[16,1,1024]{2,1,0:T(2,128)(2,1)S(1)} %constant_dynamic-slice_fusion), kind=kOutput, calls=%fused_computation.12 | convolution fusion | flops 469762048 | bytes 30310400 | tf_op jit(solution)/shard_map/bd,rdpc->bprc/dot_general | solution.py:99
  78.0 11.4 %fusion.7 = f32[16,8,2,1,896]{4,0,1,2,3:T(8,128)S(1)} fusion(bf16[2,128,8,8,896]{4,3,2,1,0:T(8,128)(2,1)} %bitcast.113, bf16[16,1,1024]{2,1,0:T(2,128)(2,1)S(1)} %constant_dynamic-slice_fusion), kind=kOutput, calls=%fused_computation.11 | convolution fusion | flops 469762048 | bytes 30310400 | tf_op jit(solution)/shard_map/bd,rdpc->bprc/dot_general | solution.py:98
  89.4 0.2 fusion.6
  89.6 1.6 collective-permute-start
  91.1 21.1 %collective-permute-done = bf16[16,8,2,2,896]{4,0,1,2,3:T(8,128)(2,1)S(1)} collective-permute-done((bf16[16,8,2,2,896]{4,0,1,2,3:T(8,128)(2,1)S(1)}, bf16[16,8,2,2,896]{4,0,1,2,3:T(8,128)(2,1)S(1)}, u32[]{:S(2)}, u32[]{:S(2)}) %collective-permute-start) | collective-permute-done | bytes 917536 | tf_op jit(solution)/shard_map/ppermute | solution.py:14
  112.2 1.1 fusion.28
  113.3 0.0 collective-permute-start.1
  113.4 0.6 reduce_max.19
  114.0 1.3 fusion.40
  115.2 1.9 fusion.38
  117.1 1.3 maximum_bitcast_fusion
  118.4 17.0 %collective-permute-done.1 = bf16[16,8,2,2,896]{4,0,1,2,3:T(8,128)(2,1)} collective-permute-done((bf16[16,8,2,2,896]{4,0,1,2,3:T(8,128)(2,1)}, bf16[16,8,2,2,896]{4,0,1,2,3:T(8,128)(2,1)}, u32[]{:S(2)}, u32[]{:S(2)}) %collective-permute-start.1) | collective-permute-done | bytes 917536 | tf_op jit(solution)/shard_map/ppermute | solution.py:14
  135.4 2.4 %fusion.13 = bf16[16,8,2,2,896]{4,0,1,2,3:T(8,128)(2,1)} fusion(bf16[16,8,2,2,896]{4,0,1,2,3:T(8,128)(2,1)} %collective-permute-done.1, bf16[16,8,2,2,896]{4,0,1,2,3:T(8,128)(2,1)S(1)} %collective-permute-done, f32[16,8,2,1,896]{4,0,1,2,3:T(8,128)S(1)} %fusion.10, f32[16,8,2,1,896]{4,0,1,2,3:T(8,128)S(1)} %fusion.7), kind=kLoop, calls=%fused_computation.13 | loop fusion | flops 2752512 | bytes 4587520 | tf_op jit(solution)/shard_map/convert_element_type | solution.py:102
  137.8 0.0 collective-permute-start.2
  137.8 21.8 %fusion.41 = (bf16[1,7168,1024]{2,1,0:T(8,128)(2,1)}, bf16[1,7168,1024]{2,1,0:T(8,128)(2,1)}) fusion(bf16[2,7168,1024]{2,1,0:T(8,128)(2,1)} %param.27), kind=kLoop, calls=%fused_computation.71 | loop fusion | bytes 58720256 | tf_op jit(solution)/shard_map/slice | solution.py:113
  159.6 20.8 %all-gather.1 = bf16[16,1,2]{2,1,0:T(2,128)(2,1)S(1)} all-gather(bf16[1,1,2]{2,1,0:T(2,128)(2,1)S(1)} %maximum_bitcast_fusion), channel_id=1, replica_groups=mesh['groups'=2,'gx'=16] {'gx'}, dimensions={0}, use_global_device_ids=true | all-gather | bytes 68 | tf_op jit(solution)/shard_map/all_gather | solution.py:93
  180.5 0.1 copy.44
  180.6 0.0 collective-permute-done.2
  180.6 1.8 convert_add_fusion
  182.4 0.3 fusion.23
  182.7 0.0 copy-start.1
  182.7 7.3 %fusion.16 = f32[16,1024]{1,0:T(8,128)S(1)} fusion(bf16[8,896,1024]{2,1,0:T(8,128)(2,1)} %bitcast.111, bf16[16,8,2,896]{3,0,1,2:T(8,128)(2,1)S(1)} %fusion.23, f32[16]{0:T(128)S(1)} %get-tuple-element.12), kind=kOutput, calls=%fused_computation.18 | convolution fusion | flops 234897408 | bytes 14975488 | tf_op jit(solution)/shard_map/bpc,pcn->bn/dot_general | solution.py:110
  190.1 1.7 copy-done.2
  191.8 2.0 fusion.18
  193.8 0.6 reduce.14
  194.4 18.1 %all_to_all.18 = bf16[16,2,512]{2,1,0:T(2,128)(2,1)S(1)} all-to-all(bf16[16,2,512]{2,1,0:T(2,128)(2,1)S(1)} %reshape.235), channel_id=1, replica_groups=mesh['groups'=2,'gx'=16] {'gx'}, dimensions={0} | all-to-all | bytes 65536 | tf_op jit(solution)/shard_map/all_to_all | solution.py:118
  212.6 0.2 convert_reduce_fusion
  212.8 0.1 reduce_sum.59
  212.9 0.7 add_convert_fusion
  (23 shorter events, 0.2 us)
Async XLA Ops:
  0.0 2.4 %copy-start = (bf16[1,8192]{1,0:T(2,128)(2,1)S(1)}, bf16[1,8192]{1,0:T(2,128)(2,1)}, u32[]{:S(2)}) copy-start(bf16[1,8192]{1,0:T(2,128)(2,1)} %param.15) | copy-start | bytes 49156
  0.0 46.0 %copy-start.3 = (bf16[1,8192]{1,0:T(2,128)(2,1)S(1)}, bf16[1,8192]{1,0:T(2,128)(2,1)}, u32[]{:S(2)}) copy-start(bf16[1,8192]{1,0:T(2,128)(2,1)} %param.14) | copy-start | bytes 49156
  0.0 47.4 %copy-start.4 = (f32[8192]{0:T(1024)S(1)}, f32[8192]{0:T(1024)}, u32[]{:S(2)}) copy-start(f32[8192]{0:T(1024)} %param.24) | copy-start | bytes 98308
  36.0 10.0 %all-to-all-start = ((bf16[16,2,256]{2,1,0:T(2,128)(2,1)}), bf16[16,2,256]{2,1,0:T(2,128)(2,1)S(1)}, u32[]{:S(2)}, u32[]{:S(2)}) async-start(bf16[16,2,256]{2,1,0:T(2,128)(2,1)} %reshape.233), calls=%async_computation | async-start | bytes 32768 | tf_op jit(solution)/shard_map/all_to_all | solution.py:82
  78.0 35.3 %copy-start.6 = (f32[1,2]{1,0:T(1,128)S(1)}, f32[1,2]{1,0:T(1,128)}, u32[]{:S(2)}) copy-start(f32[1,2]{1,0:T(1,128)} %param.22) | copy-start | bytes 28
  78.0 37.2 %copy-start.5 = (s32[1,2]{1,0:T(1,128)S(1)}, s32[1,2]{1,0:T(1,128)}, u32[]{:S(2)}) copy-start(s32[1,2]{1,0:T(1,128)} %param.21) | copy-start | bytes 28
  89.6 22.7 %collective-permute-start = (bf16[16,8,2,2,896]{4,0,1,2,3:T(8,128)(2,1)S(1)}, bf16[16,8,2,2,896]{4,0,1,2,3:T(8,128)(2,1)S(1)}, u32[]{:S(2)}, u32[]{:S(2)}) collective-permute-start(bf16[16,8,2,2,896]{4,0,1,2,3:T(8,128)(2,1)S(1)} %fusion.6), channel_id=1, source_target_pairs={{0,2},{1,3},{2,0},{3,1},{4,6},{5,7},{6,4},{7,5},{8,10},{9,11},{10,... | collective-permute-start | bytes 2752520 | tf_op jit(solution)/shard_map/ppermute | solution.py:14
  113.3 22.1 %collective-permute-start.1 = (bf16[16,8,2,2,896]{4,0,1,2,3:T(8,128)(2,1)}, bf16[16,8,2,2,896]{4,0,1,2,3:T(8,128)(2,1)}, u32[]{:S(2)}, u32[]{:S(2)}) collective-permute-start(bf16[16,8,2,2,896]{4,0,1,2,3:T(8,128)(2,1)} %fusion.28), channel_id=1, source_target_pairs={{0,4},{1,5},{2,6},{3,7},{4,0},{5,1},{6,2},{7,3},{8,12},{9,13},{10,... | collective-permute-start | bytes 2752520 | tf_op jit(solution)/shard_map/ppermute | solution.py:14
  137.8 42.8 %collective-permute-start.2 = (bf16[16,8,2,2,896]{4,0,1,2,3:T(8,128)(2,1)}, bf16[16,8,2,2,896]{4,0,1,2,3:T(8,128)(2,1)}, u32[]{:S(2)}, u32[]{:S(2)}) collective-permute-start(bf16[16,8,2,2,896]{4,0,1,2,3:T(8,128)(2,1)} %fusion.13), channel_id=1, source_target_pairs={{0,8},{1,9},{2,10},{3,11},{4,12},{5,13},{6,14},{7,15},{8,0},{9,1},... | collective-permute-start | bytes 2752520 | tf_op jit(solution)/shard_map/ppermute | solution.py:14
  182.4 9.3 %copy-start.2 = (bf16[1,7168,1024]{2,1,0:T(8,128)(2,1)S(1)}, bf16[1,7168,1024]{2,1,0:T(8,128)(2,1)}, u32[]{:S(2)}) copy-start(bf16[1,7168,1024]{2,1,0:T(8,128)(2,1)} %get-tuple-element.7) | copy-start | bytes 44040196
  182.7 30.9 %copy-start.1 = (bf16[1,8192]{1,0:T(2,128)(2,1)S(1)}, bf16[1,8192]{1,0:T(2,128)(2,1)}, u32[]{:S(2)}) copy-start(bf16[1,8192]{1,0:T(2,128)(2,1)} %param.15) | copy-start | bytes 49156
where the time goes:
time: 214 us
  blocking collectives  82.6 us (39%)
  waiting for transfers between devices  44.5 us (21%)
  matrix products  38 us (18%)
  local copies, waits for them, and re-layouts  27.1 us (13%)
  other arithmetic  14.7 us (7%)
  starting transfers between devices  5.07 us (2%)
    ppermute x3, waiting for transfers between devices, partner(): lax.ppermute(value, axis, [(i, i ^ 1 << distance) for i in range(lax.axis...  38.1 us
    all_gather x1, blocking collectives, on_device(): lax.all_gather(attn, 'gx', axis=0, tiled=True)  24.6 us
    slice x1, local copies, waits for them, and re-layouts, on_device(): down_view[expert]  21.8 us
    all_gather x1, blocking collectives, on_device(): lax.all_gather(weight, 'gx', axis=0, tiled=True)  20.8 us
    all_gather x1, blocking collectives, on_device(): lax.all_gather(normed, 'gx', axis=0, tiled=True)  19.1 us
    all_to_all x1, blocking collectives, on_device(): lax.all_to_all(partial_out.astype(jnp.bfloat16), 'gx', split_axis=0, conc...  18.1 us
    dot_general x1, matrix products, on_device(): jnp.einsum('bd,rdpc->bprc', rows_in, gate_view, preferred_element_type=jn...  11.4 us
    dot_general x1, matrix products, on_device(): jnp.einsum('bd,rdpc->bprc', rows_in, up_view, preferred_element_type=jnp....  11.4 us
  transfers between devices with their start and end apart: 4, of which 3 were waited for; matrix products, arithmetic and copies ran while one was open for 13% of the time, Pallas kernels for 0%

commit v1 on v0

--- a/solution.py
+++ b/solution.py
@@ -1,6 +1,10 @@
+import functools
+
 import jax
 import jax.numpy as jnp
 from jax import lax
+from jax.experimental import pallas as pl
+from jax.experimental.pallas import tpu as pltpu
 from jax.sharding import PartitionSpec as P
 
 NH = 64
@@ -8,6 +12,7 @@
 HS = 128
 RESIDENT = 2
 MSPLIT = 8
+HINT = 100_000_000_000
 
 
 def partner(value, axis, distance):
@@ -45,7 +50,7 @@
     return (jax.nn.silu(parts[..., 0, :]) * parts[..., 1, :]).astype(jnp.bfloat16)
 
 
-def on_device(
+def plain_on_device(
     stream_in,
     query,
     key_new,
@@ -123,6 +128,499 @@
     return (resid + ffn).astype(jnp.bfloat16)
 
 
+def lane_iota(shape):
+    return lax.broadcasted_iota(jnp.int32, shape, len(shape) - 1)
+
+
+def row_iota(shape):
+    return lax.broadcasted_iota(jnp.int32, shape, 0)
+
+
+def split_three(value):
+    high = value.astype(jnp.bfloat16)
+    rest = value - high.astype(jnp.float32)
+    mid = rest.astype(jnp.bfloat16)
+    low = (rest - mid.astype(jnp.float32)).astype(jnp.bfloat16)
+    return high, mid, low
+
+
+def one_block(kernel, outs, args, spaces, name, scratch=(), flops=0, grant=3 << 20):
+    return pl.pallas_call(
+        kernel,
+        out_shape=[jax.ShapeDtypeStruct(shape, dtype) for shape, dtype in outs],
+        in_specs=[pl.BlockSpec(memory_space=space) for space in spaces],
+        out_specs=[pl.BlockSpec(memory_space=pltpu.VMEM) for _ in outs],
+        scratch_shapes=list(scratch),
+        cost_estimate=pl.CostEstimate(flops=flops, transcendentals=0, bytes_accessed=1 << 20),
+        compiler_params=pltpu.CompilerParams(vmem_limit_bytes=grant),
+        name=name,
+    )(*args)
+
+
+def attend_kernel(*refs):
+    lengths, sources, out, places, sems, work = refs[0], refs[1:9], refs[9], refs[10:18], refs[18], refs[19:]
+    copies = [
+        pltpu.make_async_copy(source, place, sems.at[i])
+        for i, (source, place) in enumerate(zip(sources, places))
+    ]
+    for copy in copies:
+        copy.start()
+    for copy in copies:
+        copy.wait()
+    ids, scores_in, query, key_new, value_new, stream, keys, values = places
+    q_rows, s_rows, own_k, own_v, s_acc = work
+    blocks, rows = out.shape[0], out.shape[1]
+    group = NH // KVH
+    for head in range(NH):
+        q_rows[head : head + 1, :] = query[0:1, head * HS : (head + 1) * HS].astype(jnp.float32)
+    for tile in range(s_rows.shape[0]):
+        s_rows[tile : tile + 1, :] = stream[0:1, tile * HS : (tile + 1) * HS].astype(jnp.float32)
+    for g in range(KVH):
+        cut = slice(g * HS, (g + 1) * HS)
+        here = slice(g * group, (g + 1) * group)
+        own_k[here, :] = jnp.broadcast_to(key_new[0:1, cut].astype(jnp.float32), (group, HS))
+        own_v[here, :] = jnp.broadcast_to(value_new[0:1, cut].astype(jnp.float32), (group, HS))
+        s_acc[here, :] = lax.dot_general(
+            q_rows[here, :].astype(jnp.bfloat16),
+            keys[0, :, cut],
+            (((1,), (1,)), ((), ())),
+            preferred_element_type=jnp.float32,
+        )
+    scale = HS ** (-0.5)
+    scores = s_acc[...] * scale
+    scores = jnp.where(lane_iota(scores.shape) < lengths[0], scores, -1e30)
+    own = jnp.sum(q_rows[...] * own_k[...], axis=-1, keepdims=True) * scale
+    top = jnp.maximum(jnp.max(scores, axis=-1, keepdims=True), own)
+    e_cache = jnp.exp(scores - top)
+    e_own = jnp.exp(own - top)
+    total = jnp.sum(e_cache, axis=-1, keepdims=True) + e_own
+    p_cache = e_cache / total
+    p_own = (e_own / total).astype(jnp.bfloat16).astype(jnp.float32)
+    s_acc[...] = p_cache
+    for g in range(KVH):
+        cut = slice(g * HS, (g + 1) * HS)
+        here = slice(g * group, (g + 1) * group)
+        mixed = jnp.dot(
+            s_acc[here, :].astype(jnp.bfloat16), values[0, :, cut], preferred_element_type=jnp.float32
+        )
+        q_rows[here, :] = mixed + p_own[here, :] * own_v[here, :]
+    attn = q_rows[...].astype(jnp.bfloat16)
+    first = jnp.full((8, HS), scores_in[0, 0])
+    second = jnp.full((8, HS), scores_in[0, 1])
+    peak = jnp.maximum(first, second)
+    e_first = jnp.exp(first - peak)
+    e_second = jnp.exp(second - peak)
+    both = e_first + e_second
+    tail = jnp.zeros((8, HS), jnp.float32)
+    for expert in range(RESIDENT):
+        w = jnp.where(ids[0, 0] == expert, e_first / both, 0.0)
+        w = w + jnp.where(ids[0, 1] == expert, e_second / both, 0.0)
+        tail = jnp.where(row_iota(tail.shape) == expert, w, tail)
+    tail = tail.astype(jnp.bfloat16)
+    per = s_rows.shape[0] // blocks
+    for block in range(blocks):
+        out[block, 0:NH, :] = attn
+        out[block, NH : NH + per, :] = s_rows[block * per : (block + 1) * per, :].astype(jnp.bfloat16)
+        out[block, NH + per : rows, :] = tail
+
+
+def project_kernel(weight, gathered, gain, out, resid_out, slot_out, pick_out, rows32, lhs, acc, *, slots):
+    batch, width = acc.shape
+    rows = gathered.shape[2]
+    half = lax.axis_index("gx") % 2
+    place = lax.axis_index("gx")
+    rows32[...] = gathered[...].reshape(batch * rows, HS).astype(jnp.float32)
+    for head in range(NH):
+        lhs[:, head * HS : (head + 1) * HS] = rows32[pl.ds(head, batch, stride=rows), :].astype(jnp.bfloat16)
+    acc[...] = jnp.dot(lhs[...], weight[...], preferred_element_type=jnp.float32)
+    per = width // HS
+    power = jnp.zeros((batch, 1), jnp.float32)
+    for q in range(per):
+        cut = slice(q * HS, (q + 1) * HS)
+        stream = rows32[pl.ds(NH + half * per + q, batch, stride=rows), :]
+        resid = stream + acc[:, cut].astype(jnp.bfloat16).astype(jnp.float32)
+        resid_out[:, cut] = resid
+        power = power + jnp.sum(resid * resid, axis=-1, keepdims=True)
+        scaled = resid * gain[pl.ds(place * per + q, 1), :]
+        out[:, cut] = scaled.astype(jnp.bfloat16)
+    lanes = lane_iota((batch, HS))
+    high, mid, low = split_three(jnp.broadcast_to(power, (batch, HS)))
+    zero = jnp.zeros((batch, HS), jnp.float32)
+    packed = jnp.where(lanes == 0, high.astype(jnp.float32), zero)
+    packed = jnp.where(lanes == 1, mid.astype(jnp.float32), packed)
+    packed = jnp.where(lanes == 2, low.astype(jnp.float32), packed)
+    out[:, width : width + HS] = packed.astype(jnp.bfloat16)
+    tri = (lane_iota((batch, batch)) < row_iota((batch, batch))).astype(jnp.bfloat16)
+    onehot = jnp.zeros((batch, HS), jnp.float32)
+    picked = jnp.zeros((batch, HS), jnp.float32)
+    for expert in range(RESIDENT):
+        w = rows32[pl.ds(NH + 2 * per + expert, batch, stride=rows), :]
+        named = w > 0.0
+        rank = jnp.dot(tri, named.astype(jnp.bfloat16), preferred_element_type=jnp.float32)
+        slot = lanes.astype(jnp.float32)
+        for turn, low_edge in enumerate((expert * 16 + expert * slots % 8, 32 + expert * slots)):
+            inside = (lanes >= low_edge) & (lanes < low_edge + slots)
+            hit = inside & named & (rank + float(low_edge) == slot)
+            onehot = jnp.where(hit, 1.0, onehot)
+            if turn == 0:
+                picked = jnp.where(hit, w, picked)
+    slot_out[...] = onehot
+    pick_out[...] = picked
+
+
+def merged(left, right):
+    return jnp.concatenate([left[:8], left[8:] + right[:8], right[8:]], axis=0)
+
+
+class UpBlocks:
+    def __init__(self, up, ring, sems, side):
+        self.up, self.ring, self.sems, self.side = up, ring, sems, side
+        self.depth, self.rows, self.narrow = ring.shape
+        self.pieces = up.shape[1] // self.rows
+        self.total = 4 * RESIDENT * self.pieces
+        for k in range(self.depth):
+            self.copy(k).start()
+
+    def columns(self, z, side):
+        return pl.ds(pl.multiple_of((2 * z + side) * self.narrow, HS), self.narrow)
+
+    def copy(self, k):
+        slot = k % self.depth
+        block, piece = k // self.pieces, k % self.pieces
+        source = self.up.at[
+            block % RESIDENT,
+            piece * self.rows : (piece + 1) * self.rows,
+            self.columns(block // RESIDENT, self.side),
+        ]
+        return pltpu.make_async_copy(source, self.ring.at[slot], self.sems.at[slot])
+
+    def times(self, lhs, z, expert):
+        result = None
+        for piece in range(self.pieces):
+            k = (z * RESIDENT + expert) * self.pieces + piece
+            self.copy(k).wait()
+            cut = slice(piece * self.rows, (piece + 1) * self.rows)
+            term = jnp.dot(lhs[expert, :, cut], self.ring[k % self.depth], preferred_element_type=jnp.float32)
+            result = term if result is None else result + term
+            if k + self.depth < self.total:
+                self.copy(k + self.depth).start()
+        return result
+
+
+def stacked(work, gate, up, half):
+    work[0:half, :] = gate[:half]
+    work[half : 2 * half, :] = up[:half]
+
+
+def gate_kernel(mine, other, onehot, gate, up, out, gate_out, lhs_out, place_out, tail_out, ring, sems, work, *, slots):
+    batch = mine.shape[0]
+    place = lax.axis_index("gx")
+    side = place // 2 % 2
+    blocks = UpBlocks(up, ring, sems, 1 - side)
+    lines = 2 * RESIDENT * slots
+    width = mine.shape[1] - HS
+    first = place % 2 == 0
+    own = mine[:, :width].astype(jnp.float32)
+    far = other[:, :width].astype(jnp.float32)
+    left = jnp.where(first, own, far).astype(jnp.bfloat16)
+    right = jnp.where(first, far, own).astype(jnp.bfloat16)
+    hot = onehot[...].astype(jnp.bfloat16)
+    over = (((0,), (0,)), ((), ()))
+    for at, piece in ((0, left), (width, right)):
+        spread = lax.dot_general(hot[:, : RESIDENT * 16], piece, over, preferred_element_type=jnp.float32)
+        for expert in range(RESIDENT):
+            lhs_out[expert, :, at : at + width] = spread[expert * 16 : (expert + 1) * 16].astype(jnp.bfloat16)
+    power = mine[:, width:].astype(jnp.float32) + other[:, width:].astype(jnp.float32)
+    power = jnp.sum(power, axis=-1, keepdims=True)
+    eye = lane_iota((batch, HS)) == row_iota((batch, HS))
+    line = jnp.sum(jnp.where(eye, power, 0.0), axis=0, keepdims=True)
+    high, mid, low = split_three(line)
+    rows = row_iota((8, HS))
+    tail = jnp.where(rows == 0, high.astype(jnp.float32), 0.0)
+    tail = jnp.where(rows == 1, mid.astype(jnp.float32), tail)
+    tail = jnp.where(rows == 2, low.astype(jnp.float32), tail)
+    tail_out[...] = tail
+    hot_rows = hot[:, 32 : 32 + place_out.shape[0]]
+    place_out[...] = lax.dot_general(hot_rows, eye.astype(jnp.bfloat16), over, preferred_element_type=jnp.float32)
+    narrow = blocks.narrow
+    half = RESIDENT * slots
+
+    for z in range(out.shape[0]):
+        out[z, out.shape[1] - 8 :, :] = tail.astype(jnp.bfloat16)
+        cut = slice(2 * z * narrow, 2 * (z + 1) * narrow)
+        gates = merged(
+            *[jnp.dot(lhs_out[expert], gate[expert, :, cut], preferred_element_type=jnp.float32) for expert in range(RESIDENT)]
+        )
+        lower, upper = gates[:, :narrow], gates[:, narrow:]
+        gate_out[z] = jnp.where(side == 0, lower, upper)
+        ups = [blocks.times(lhs_out, z, expert) for expert in range(RESIDENT)]
+        stacked(work, jnp.where(side == 0, upper, lower), merged(*ups), half)
+        for q in range(narrow // HS):
+            out[z, q * lines : (q + 1) * lines, :] = work[:, q * HS : (q + 1) * HS].astype(jnp.bfloat16)
+
+
+def up_kernel(lhs, tail, gate_sums, up, out, ring, sems, work, *, slots):
+    side = lax.axis_index("gx") // 2 % 2
+    blocks = UpBlocks(up, ring, sems, side)
+    lines = 2 * RESIDENT * slots
+    half = RESIDENT * slots
+    for z in range(out.shape[0]):
+        out[z, out.shape[1] - 8 :, :] = tail[...]
+        ups = [blocks.times(lhs, z, expert) for expert in range(RESIDENT)]
+        stacked(work, gate_sums[z], merged(*ups), half)
+        for q in range(blocks.narrow // HS):
+            out[z, q * lines : (q + 1) * lines, :] = work[:, q * HS : (q + 1) * HS]
+
+
+def pair_kernel(near_sums, got, keep, *sends):
+    z = lax.axis_index("gx") // 4
+    keep[...] = near_sums[z] + got[z].astype(jnp.float32)
+    for d, send in enumerate(sends, 1):
+        send[...] = (near_sums[z ^ d] + got[z ^ d].astype(jnp.float32)).astype(jnp.bfloat16)
+
+
+def gated_kernel(keep, first, second, third, place, out, work, packed, *, slots, width):
+    lines = 2 * RESIDENT * slots
+    blocks = out.shape[0]
+    per = (keep.shape[0] - 8) // lines
+    total = keep[...]
+    for got in (first, second, third):
+        total = total + got[...].astype(jnp.float32)
+    work[...] = total
+    line = jnp.sum(work[per * lines : per * lines + 8, :], axis=0, keepdims=True)
+    inverse = lax.rsqrt(line / width + 1e-05)
+    factor = jnp.sum(place[...] * inverse, axis=-1, keepdims=True)
+    half = RESIDENT * slots
+    scale = factor[:half, :]
+    packed[packed.shape[0] - 8 :, :] = jnp.zeros((8, HS), jnp.float32)
+    for q in range(per):
+        gate = work[q * lines : q * lines + half, :] * scale
+        up = work[q * lines + half : (q + 1) * lines, :] * scale
+        packed[q * half : (q + 1) * half, :] = gate / (1.0 + jnp.exp(-gate)) * up
+    hidden = packed[...].astype(jnp.bfloat16)
+    for block in range(blocks):
+        out[block] = hidden
+
+
+def down_kernel(hidden, down, picked, resid, out, spread, rows32, lhs, acc, *, slots):
+    blocks = hidden.shape[0]
+    half = lax.axis_index("gx") % 2
+    each = RESIDENT * slots
+    per = lhs.shape[2] // blocks // HS
+    for block in range(blocks):
+        rows32[block] = hidden[block].astype(jnp.float32)
+        for q in range(per):
+            at = (block * per + q) * HS
+            for expert in range(RESIDENT):
+                start = q * each + expert * slots // 8 * 8
+                lhs[expert, :, at : at + HS] = rows32[block, start : start + 16, :].astype(jnp.bfloat16)
+    tile = acc.shape[1] // 2
+
+    def columns(k, carry):
+        cut = pl.ds(pl.multiple_of(k * tile, tile), tile)
+        for expert in range(RESIDENT):
+            acc[expert * 16 : (expert + 1) * 16, cut] = jnp.dot(
+                lhs[expert], down[expert, :, cut], preferred_element_type=jnp.float32
+            )
+        return carry
+
+    lax.fori_loop(0, 2, columns, 0)
+    weight = picked[...].astype(jnp.bfloat16)[:, : RESIDENT * 16]
+    result = None
+    for part in split_three(acc[...]):
+        term = jnp.dot(weight, part, preferred_element_type=jnp.float32)
+        result = term if result is None else result + term
+    own = resid[...]
+    none = jnp.zeros_like(own)
+    width = own.shape[1]
+    result = result + jnp.concatenate(
+        [jnp.where(half == 0, own, none), jnp.where(half == 0, none, own)], axis=1
+    )
+    tiles = result.shape[1] // HS
+    for q in range(tiles):
+        for h in range(2):
+            spread[pl.ds(h * tiles + q, blocks, stride=2 * tiles), :] = result[
+                h * blocks : (h + 1) * blocks, q * HS : (q + 1) * HS
+            ]
+    out[...] = spread[...].reshape(out.shape).astype(jnp.bfloat16)
+
+
+def finish_kernel(got, out):
+    blocks = got.shape[0] // 2
+    per = got.shape[1]
+    for block in range(blocks):
+        total = got[2 * block].astype(jnp.float32) + got[2 * block + 1].astype(jnp.float32)
+        for q in range(per):
+            at = (block * per + q) * HS
+            out[0:1, at : at + HS] = total[q : q + 1, :].astype(jnp.bfloat16)
+
+
+def fast_on_device(
+    stream_in,
+    query,
+    key_new,
+    value_new,
+    key_cache,
+    value_cache,
+    lengths,
+    route_ids,
+    route_scores,
+    out_weight,
+    norm_gain,
+    gate_weight,
+    up_weight,
+    down_weight,
+):
+    width = stream_in.shape[1]
+    members = lax.axis_size("gx")
+    batch = members
+    own_width = width // members
+    block_width = width // MSPLIT
+    hidden_cols = gate_weight.shape[2]
+    slots = 5 * batch // 8
+    lines = 2 * RESIDENT * slots
+    bf16, f32 = jnp.bfloat16, jnp.float32
+    chips = [[2 * chip + core for chip in range(MSPLIT)] for core in range(2)]
+    cores = [[2 * chip, 2 * chip + 1] for chip in range(MSPLIT)]
+    swap = [(i, i ^ 1) for i in range(members)]
+    V = pltpu.VMEM
+
+    def near(value):
+        return pltpu.with_memory_space_constraint(value, V)
+
+    rows = NH + block_width // HS + 8
+
+    def exchange(value, groups):
+        return lax.all_to_all(
+            value, "gx", split_axis=0, concat_axis=0, tiled=True, axis_index_groups=groups
+        )
+
+    loaded = (route_ids, route_scores, query, key_new, value_new, stream_in, key_cache, value_cache)
+    (sent,) = one_block(
+        attend_kernel,
+        [((MSPLIT, rows, HS), bf16)],
+        [lengths] + [pltpu.with_memory_space_constraint(value, pltpu.HBM) for value in loaded],
+        [pltpu.SMEM] + [pltpu.HBM] * len(loaded),
+        "attend",
+        scratch=[(pltpu.SMEM if i < 2 else pltpu.VMEM)(value.shape, value.dtype) for i, value in enumerate(loaded)]
+        + [pltpu.SemaphoreType.DMA((len(loaded),))]
+        + [
+            pltpu.VMEM((NH, HS), f32),
+            pltpu.VMEM((width // HS, HS), f32),
+            pltpu.VMEM((NH, HS), f32),
+            pltpu.VMEM((NH, HS), f32),
+            pltpu.VMEM((NH, HS), f32),
+        ],
+        flops=HINT,
+    )
+    chip_rows = exchange(sent, chips)
+    gathered = lax.all_gather(chip_rows, "gx", axis=0, tiled=False, axis_index_groups=cores)
+    mine, resid, onehot, picked = one_block(
+        functools.partial(project_kernel, slots=slots),
+        [((batch, own_width + HS), bf16), ((batch, own_width), f32), ((batch, HS), f32), ((batch, HS), f32)],
+        (near(out_weight), gathered, norm_gain.reshape(width // HS, HS)),
+        [V, V, V],
+        "project",
+        scratch=[
+            pltpu.VMEM((batch * rows, HS), f32),
+            pltpu.VMEM((batch, width), bf16),
+            pltpu.VMEM((batch, own_width), f32),
+        ],
+    )
+    other = lax.ppermute(mine, "gx", swap)
+    narrow = hidden_cols // MSPLIT
+    per = narrow // HS
+    held = -(-RESIDENT * slots // 8) * 8
+    chunk = (per * lines + 8, HS)
+    flat = (-(-per * RESIDENT * slots // 8) * 8, HS)
+    up_hbm = pltpu.with_memory_space_constraint(up_weight, pltpu.HBM)
+
+    def side_scratch(depth):
+        return [
+            pltpu.VMEM((depth, block_width // 2, narrow), bf16),
+            pltpu.SemaphoreType.DMA((depth,)),
+            pltpu.VMEM((lines, narrow), f32),
+        ]
+
+    far, gate_sums, lhs, place, tail = one_block(
+        functools.partial(gate_kernel, slots=slots),
+        [
+            ((4,) + chunk, bf16),
+            ((4, held, narrow), f32),
+            ((RESIDENT, 16, block_width), bf16),
+            ((held, HS), f32),
+            ((8, HS), f32),
+        ],
+        (near(mine), near(other), near(onehot), near(gate_weight), up_hbm),
+        [V, V, V, V, pltpu.HBM],
+        "gate",
+        scratch=side_scratch(6),
+        grant=7 << 20,
+    )
+    crossed = lax.ppermute(far, "gx", [(i, i ^ 2) for i in range(members)])
+    (near_sums,) = one_block(
+        functools.partial(up_kernel, slots=slots),
+        [((4,) + chunk, f32)],
+        (lhs, tail, gate_sums, up_hbm),
+        [V, V, V, pltpu.HBM],
+        "up",
+        scratch=side_scratch(7),
+        grant=8 << 20,
+    )
+    keep, *sends = one_block(
+        pair_kernel, [(chunk, f32)] + [(chunk, bf16)] * 3, (near_sums, crossed), [V, V], "pair"
+    )
+    got = [lax.ppermute(sends[d - 1], "gx", [(i, i ^ 4 * d) for i in range(members)]) for d in (1, 2, 3)]
+    (hidden,) = one_block(
+        functools.partial(gated_kernel, slots=slots, width=width),
+        [((MSPLIT,) + flat, bf16)],
+        (keep, *got, place),
+        [V] * 5,
+        "gated",
+        scratch=[pltpu.VMEM(chunk, f32), pltpu.VMEM(flat, f32)],
+        flops=HINT,
+    )
+    hidden_all = exchange(hidden, chips)
+    (partial_out,) = one_block(
+        functools.partial(down_kernel, slots=slots),
+        [((members, block_width // HS, HS), bf16)],
+        (hidden_all, near(down_weight), picked, resid),
+        [V, V, V, V],
+        "down",
+        scratch=[
+            pltpu.VMEM((members * block_width // HS, HS), f32),
+            pltpu.VMEM((MSPLIT,) + flat, f32),
+            pltpu.VMEM((RESIDENT, 16, hidden_cols), bf16),
+            pltpu.VMEM((RESIDENT * 16, block_width), f32),
+        ],
+    )
+    last = exchange(partial_out, None)
+    (out,) = one_block(finish_kernel, [((1, width), bf16)], (last,), [V], "finish")
+    return out
+
+
+def fits(shapes, members):
+    width = shapes[0][1]
+    hidden_cols = shapes[11][2]
+    return (
+        members == 2 * MSPLIT
+        and shapes[0][0] == 1
+        and shapes[4][1] == HS
+        and width == NH * HS
+        and width % (members * HS) == 0
+        and hidden_cols % (MSPLIT * HS) == 0
+        and (5 * members) % 8 == 0
+        and 8 <= 5 * members // 8 <= 14
+        and RESIDENT == 2
+    )
+
+
+def on_device(*args):
+    if fits([arg.shape for arg in args], lax.axis_size("gx")):
+        return fast_on_device(*args)
+    return plain_on_device(*args)
+
+
 def solution(mesh):
     return jax.shard_map(
         on_device,

time: 214 us -> 76.2 us (0.36)
  blocking collectives: 82.6 us -> 38.8 us
  matrix products: 38 us -> 0 us
  waiting for transfers between devices: 44.5 us -> 7.14 us
  local copies, waits for them, and re-layouts: 27.1 us -> 0.04 us
  Pallas kernels: 0 us -> 23.5 us
  other arithmetic: 14.7 us -> 0.01 us
    all_gather x3 -> x1, blocking collectives: 64.5 us -> 2.03 us  [fast_on_device(): lax.all_gather(chip_rows, 'gx', axis=0, tiled=False, axis_index_groups=co...]
    dot_general x8 -> x0, matrix products: 38 us -> none  [the longest x1 11.4 us: on_device(): jnp.einsum('bd,rdpc->bprc', rows_in, gate_view, preferred_element_type=jn...]
    ppermute x3 -> x5, waiting for transfers between devices: 38.1 us -> 7.14 us  [the longest x3 4.02 us: fast_on_device(): lax.ppermute(sends[d - 1], 'gx', [(i, i ^ 4 * d) for i in range(members)])]
    pallas_call x0 -> x8, Pallas kernels: none -> 23.5 us  [one_block(): pl.pallas_call(kernel, out_shape=[jax.ShapeDtypeStruct(shape, dtype) for...]
    slice x1 -> x0, local copies, waits for them, and re-layouts: 21.8 us -> none  [on_device(): down_view[expert]]
    all_to_all x1 -> x3, blocking collectives: 18.1 us -> 36.8 us  [exchange(): lax.all_to_all(value, 'gx', split_axis=0, concat_axis=0, tiled=True, axis...]
    all_to_all x1 -> x0, waiting for transfers between devices: 6.45 us -> none  [on_device(): lax.all_to_all(proj_cols, 'gx', split_axis=0, concat_axis=1, tiled=True)]
    convert_element_type x8 -> x0, other arithmetic: 5.95 us -> none  [the longest x3 3.65 us: on_device(): parts.astype(jnp.bfloat16)]
  transfers between devices with their start and end apart: 4 -> 5, of which waited for: 3 -> 4; matrix products, arithmetic and copies ran while one was open for 13% -> 0% of each run, Pallas kernels for 0% -> 8%
where the time goes in v1:
time: 76.2 us; the launch traced here: 75.9 us
  blocking collectives  38.8 us (51%)
  Pallas kernels  23.5 us (31%)
  waiting for transfers between devices  7.14 us (9%)
  starting transfers between devices  5.63 us (7%)
  between operations  0.8 us (1%)
    all_to_all x3, blocking collectives, exchange(): lax.all_to_all(value, 'gx', split_axis=0, concat_axis=0, tiled=True, axis...  36.8 us
    pallas_call x8, Pallas kernels, one_block(): pl.pallas_call(kernel, out_shape=[jax.ShapeDtypeStruct(shape, dtype) for...  23.5 us
    ppermute x3, starting transfers between devices, fast_on_device(): lax.ppermute(sends[d - 1], 'gx', [(i, i ^ 4 * d) for i in range(members)])  4.45 us
    ppermute x3, waiting for transfers between devices, fast_on_device(): lax.ppermute(sends[d - 1], 'gx', [(i, i ^ 4 * d) for i in range(members)])  4.02 us
    ppermute x1, waiting for transfers between devices, fast_on_device(): crossed = lax.ppermute(far, 'gx', [(i, i ^ 2) for i in range(members)])  2.07 us
    all_gather x1, blocking collectives, fast_on_device(): lax.all_gather(chip_rows, 'gx', axis=0, tiled=False, axis_index_groups=co...  2.03 us
  transfers between devices with their start and end apart: 5, of which 4 were waited for; matrix products, arithmetic and copies ran while one was open for 0% of the time, Pallas kernels for 8%

profile of v1, /device:TPU:0, one launch (start us, length us, event | category | flops | bytes accessed | tf_op | source)
XLA Modules:
  0.0 75.9 jit_solution(16491063035481423459)
XLA Ops:
  0.7 0.0 copy-start.1
  0.7 0.0 copy-start.2
  0.7 0.0 copy-start
  0.7 1.9 %attend.1 = bf16[8,80,128]{2,1,0:T(8,128)(2,1)S(1)} custom-call(s32[1]{0:T(128)S(6)} %copy.15.refs_0_, s32[1,2]{1,0:T(1,128)} %refs_1_.1, f32[1,2]{1,0:T(1,128)} %refs_2_.1, bf16[1,8192]{1,0:T(2,128)(2,1)} %refs_3_.1, bf16[1,1024]{1,0:T(2,128)(2,1)} %refs_4_.1, bf16[1,1024]{1,0:T(2,128)(2,1)} %refs_5_.1, bf16[1,8192]{1,0:T(2,128)(2,1)} %refs_6_.1, ...), custom_call_target="tpu_custom_call" | custom-call | flops 99999997952 | bytes 1048576 | tf_op jit(solution)/shard_map/attend/pallas_call | solution.py:148
  2.5 14.9 %all_to_all.15 = bf16[8,80,128]{2,1,0:T(8,128)(2,1)S(1)} all-to-all(bf16[8,80,128]{2,1,0:T(8,128)(2,1)S(1)} %attend.1), channel_id=1, replica_groups={{0,2,4,6,8,10,12,14},{1,3,5,7,9,11,13,15},{16,18,20,22,24,26,28,30},{17..., dimensions={0} | all-to-all | bytes 327680 | tf_op jit(solution)/shard_map/all_to_all | solution.py:494
  17.4 2.0 %all-gather = bf16[16,80,128]{2,1,0:T(8,128)(2,1)S(1)} all-gather(bf16[8,80,128]{2,1,0:T(8,128)(2,1)S(1)} %all_to_all.15), channel_id=2, replica_groups={{0,1},{2,3},{4,5},{6,7},{8,9},{10,11},{12,13},{14,15},{16,17},{18,19},{..., dimensions={0}, use_global_device_ids=true | all-gather | bytes 491520 | tf_op jit(solution)/shard_map/all_gather | solution.py:517
  19.5 0.0 copy-done.1
  19.5 0.0 copy-done.2
  19.5 1.4 %project.1 = (bf16[16,640]{1,0:T(8,128)(2,1)S(1)}, f32[16,512]{1,0:T(8,128)S(1)}, f32[16,128]{1,0:T(8,128)S(1)}, f32[16,128]{1,0:T(8,128)S(1)}) custom-call(bf16[8192,512]{1,0:T(8,128)(2,1)S(1)} %copy-done.1, bf16[2,8,80,128]{3,2,1,0:T(8,128)(2,1)S(1)} %bitcast.4, f32[64,128]{1,0:T(8,128)S(1)} %bitcast.5), custom_call_target="tpu_custom_call" | custom-call | bytes 1048576 | tf_op jit(solution)/shard_map/project/pallas_call | solution.py:148
  20.9 0.2 collective-permute-start
  21.1 1.1 %collective-permute-done.other = bf16[16,640]{1,0:T(8,128)(2,1)S(1)} collective-permute-done((bf16[16,640]{1,0:T(8,128)(2,1)S(1)}, bf16[16,640]{1,0:T(8,128)(2,1)S(1)}, u32[]{:S(2)}, u32[]{:S(2)}) %collective-permute-start) | collective-permute-done | bytes 20512 | tf_op jit(solution)/shard_map/ppermute | solution.py:530
  22.1 0.0 copy-done
  22.1 9.0 %gate.2 = (bf16[4,288,128]{2,1,0:T(8,128)(2,1)S(1)}, f32[4,24,896]{2,1,0:T(8,128)S(1)}, bf16[2,16,1024]{2,1,0:T(8,128)(2,1)S(1)}, f32[24,128]{1,0:T(8,128)S(1)}, f32[8,128]{1,0:T(8,128)S(1)}) custom-call(bf16[16,640]{1,0:T(8,128)(2,1)S(1)} %get-tuple-element.18.mine, bf16[16,640]{1,0:T(8,128)(2,1)S(1)} %collective-permute-done.other, ...), custom_call_target="tpu_custom_call" | custom-call | bytes 1048576 | tf_op jit(solution)/shard_map/gate/pallas_call | solution.py:148
  31.1 1.0 %collective-permute-start.1 = (bf16[4,288,128]{2,1,0:T(8,128)(2,1)S(1)}, bf16[4,288,128]{2,1,0:T(8,128)(2,1)S(1)}, u32[]{:S(2)}, u32[]{:S(2)}) collective-permute-start(bf16[4,288,128]{2,1,0:T(8,128)(2,1)S(1)} %get-tuple-element.23), channel_id=1, source_target_pairs={{0,2},{1,3},{2,0},{3,1},{4,6},{5,7},{6,4},{7,5},{8,10},{9,11},{10,... | collective-permute-start | bytes 884744 | tf_op jit(solution)/shard_map/ppermute | solution.py:560
  32.1 0.0 slice-start
  32.1 6.1 %up.4.near_sums = f32[4,288,128]{2,1,0:T(8,128)S(1)} custom-call(bf16[2,16,1024]{2,1,0:T(8,128)(2,1)S(1)} %get-tuple-element.20.lhs, f32[8,128]{1,0:T(8,128)S(1)} %get-tuple-element.21.tail, f32[4,24,896]{2,1,0:T(8,128)S(1)} %get-tuple-element.22.gate_sums, bf16[2,1024,7168]{2,1,0:T(8,128)(2,1)} %up.5), custom_call_target="tpu_custom_call" | custom-call | bytes 1048576 | tf_op jit(solution)/shard_map/up/pallas_call | solution.py:148
  38.2 2.1 %collective-permute-done.1.got = bf16[4,288,128]{2,1,0:T(8,128)(2,1)S(1)} collective-permute-done((bf16[4,288,128]{2,1,0:T(8,128)(2,1)S(1)}, bf16[4,288,128]{2,1,0:T(8,128)(2,1)S(1)}, u32[]{:S(2)}, u32[]{:S(2)}) %collective-permute-start.1) | collective-permute-done | bytes 294944 | tf_op jit(solution)/shard_map/ppermute | solution.py:560
  40.3 0.1 pair.1
  40.4 0.3 collective-permute-start.2
  40.7 1.0 %collective-permute-start.3 = (bf16[288,128]{1,0:T(8,128)(2,1)S(1)}, bf16[288,128]{1,0:T(8,128)(2,1)S(1)}, u32[]{:S(2)}, u32[]{:S(2)}) collective-permute-start(bf16[288,128]{1,0:T(8,128)(2,1)S(1)} %get-tuple-element.26), channel_id=1, source_target_pairs={{0,8},{1,9},{2,10},{3,11},{4,12},{5,13},{6,14},{7,15},{8,0},{9,1},... | collective-permute-start | bytes 221192 | tf_op jit(solution)/shard_map/ppermute | solution.py:573
  41.7 3.2 %collective-permute-start.4 = (bf16[288,128]{1,0:T(8,128)(2,1)S(1)}, bf16[288,128]{1,0:T(8,128)(2,1)S(1)}, u32[]{:S(2)}, u32[]{:S(2)}) collective-permute-start(bf16[288,128]{1,0:T(8,128)(2,1)S(1)} %get-tuple-element.27), channel_id=1, source_target_pairs={{0,12},{1,13},{2,14},{3,15},{4,8},{5,9},{6,10},{7,11},{8,4},{9,5},... | collective-permute-start | bytes 221192 | tf_op jit(solution)/shard_map/ppermute | solution.py:573
  44.8 0.1 collective-permute-done.2.first
  44.9 3.9 %collective-permute-done.3.second = bf16[288,128]{1,0:T(8,128)(2,1)S(1)} collective-permute-done((bf16[288,128]{1,0:T(8,128)(2,1)S(1)}, bf16[288,128]{1,0:T(8,128)(2,1)S(1)}, u32[]{:S(2)}, u32[]{:S(2)}) %collective-permute-start.3) | collective-permute-done | bytes 73760 | tf_op jit(solution)/shard_map/ppermute | solution.py:573
  48.8 0.0 collective-permute-done.4.third
  48.8 0.0 slice-start.1
  48.8 0.0 slice-start.2
  48.8 0.0 slice-start.3
  48.8 0.0 slice-start.4
  48.9 0.0 slice-start.5
  48.9 0.0 slice-start.6
  48.9 0.2 gated.1
  49.0 12.7 %all_to_all.16.hidden = bf16[8,144,128]{2,1,0:T(8,128)(2,1)S(1)} all-to-all(bf16[8,144,128]{2,1,0:T(8,128)(2,1)S(1)} %gated.1), channel_id=1, replica_groups={{0,2,4,6,8,10,12,14},{1,3,5,7,9,11,13,15},{16,18,20,22,24,26,28,30},{17..., dimensions={0} | all-to-all | bytes 589824 | tf_op jit(solution)/shard_map/all_to_all | solution.py:494
  61.7 0.0 slice-done
  61.7 0.0 slice-done.1
  61.7 0.0 slice-done.2
  61.7 0.0 slice-done.3
  61.7 0.0 slice-done.4
  61.8 0.0 slice-done.5
  61.8 0.0 slice-done.6
  61.8 4.3 %down.2 = bf16[16,8,128]{2,1,0:T(8,128)(2,1)S(1)} custom-call(bf16[8,144,128]{2,1,0:T(8,128)(2,1)S(1)} %all_to_all.16.hidden, bf16[2,7168,1024]{2,1,0:T(8,128)(2,1)S(1)} %bitcast.3, f32[16,128]{1,0:T(8,128)S(1)} %get-tuple-element.29.picked, f32[16,512]{1,0:T(8,128)S(1)} %get-tuple-element.30.resid), custom_call_target="tpu_custom_call" | custom-call | bytes 1048576 | tf_op jit(solution)/shard_map/down/pallas_call | solution.py:148
  66.1 9.2 %all_to_all.17.got = bf16[16,8,128]{2,1,0:T(8,128)(2,1)S(1)} all-to-all(bf16[16,8,128]{2,1,0:T(8,128)(2,1)S(1)} %down.2), channel_id=1, replica_groups=mesh['groups'=2,'gx'=16] {'gx'}, dimensions={0} | all-to-all | bytes 65536 | tf_op jit(solution)/shard_map/all_to_all | solution.py:494
  75.3 0.6 finish.1
  (1 shorter events, 0.0 us)
Async XLA Ops:
  0.7 18.8 %copy-start.1 = (bf16[8192,512]{1,0:T(8,128)(2,1)S(1)}, bf16[8192,512]{1,0:T(8,128)(2,1)}, u32[]{:S(2)}) copy-start(bf16[8192,512]{1,0:T(8,128)(2,1)} %weight.1) | copy-start | bytes 25165828
  0.7 18.8 %copy-start.2 = (f32[8192]{0:T(1024)S(1)}, f32[8192]{0:T(1024)}, u32[]{:S(2)}) copy-start(f32[8192]{0:T(1024)} %param.24) | copy-start | bytes 98308
  0.7 21.4 %copy-start = (bf16[2,1024,7168]{2,1,0:T(8,128)(2,1)S(1)}, bf16[2,1024,7168]{2,1,0:T(8,128)(2,1)}, u32[]{:S(2)}) copy-start(bf16[2,1024,7168]{2,1,0:T(8,128)(2,1)} %gate.3) | copy-start | bytes 88080384
  20.9 1.3 %collective-permute-start = (bf16[16,640]{1,0:T(8,128)(2,1)S(1)}, bf16[16,640]{1,0:T(8,128)(2,1)S(1)}, u32[]{:S(2)}, u32[]{:S(2)}) collective-permute-start(bf16[16,640]{1,0:T(8,128)(2,1)S(1)} %get-tuple-element.18.mine), channel_id=1, source_target_pairs={{0,1},{1,0},{2,3},{3,2},{4,5},{5,4},{6,7},{7,6},{8,9},{9,8},{10,11... | collective-permute-start | bytes 61448 | tf_op jit(solution)/shard_map/ppermute | solution.py:530
  31.1 9.1 %collective-permute-start.1 = (bf16[4,288,128]{2,1,0:T(8,128)(2,1)S(1)}, bf16[4,288,128]{2,1,0:T(8,128)(2,1)S(1)}, u32[]{:S(2)}, u32[]{:S(2)}) collective-permute-start(bf16[4,288,128]{2,1,0:T(8,128)(2,1)S(1)} %get-tuple-element.23), channel_id=1, source_target_pairs={{0,2},{1,3},{2,0},{3,1},{4,6},{5,7},{6,4},{7,5},{8,10},{9,11},{10,... | collective-permute-start | bytes 884744 | tf_op jit(solution)/shard_map/ppermute | solution.py:560
  32.1 29.6 %slice-start = ((s8[29360128]{0:T(1024)(128)(4,1)}), s8[4194304]{0:T(1024)(128)(4,1)S(1)}, s32[]{:S(2)}) async-start(s8[29360128]{0:T(1024)(128)(4,1)} %bitcast.2), calls=%async_computation.3 | async-start | bytes 8388608
  40.4 4.5 %collective-permute-start.2 = (bf16[288,128]{1,0:T(8,128)(2,1)S(1)}, bf16[288,128]{1,0:T(8,128)(2,1)S(1)}, u32[]{:S(2)}, u32[]{:S(2)}) collective-permute-start(bf16[288,128]{1,0:T(8,128)(2,1)S(1)} %get-tuple-element.25), channel_id=1, source_target_pairs={{0,4},{1,5},{2,6},{3,7},{4,0},{5,1},{6,2},{7,3},{8,12},{9,13},{10,... | collective-permute-start | bytes 221192 | tf_op jit(solution)/shard_map/ppermute | solution.py:573
  40.7 8.2 %collective-permute-start.3 = (bf16[288,128]{1,0:T(8,128)(2,1)S(1)}, bf16[288,128]{1,0:T(8,128)(2,1)S(1)}, u32[]{:S(2)}, u32[]{:S(2)}) collective-permute-start(bf16[288,128]{1,0:T(8,128)(2,1)S(1)} %get-tuple-element.26), channel_id=1, source_target_pairs={{0,8},{1,9},{2,10},{3,11},{4,12},{5,13},{6,14},{7,15},{8,0},{9,1},... | collective-permute-start | bytes 221192 | tf_op jit(solution)/shard_map/ppermute | solution.py:573
  41.7 7.2 %collective-permute-start.4 = (bf16[288,128]{1,0:T(8,128)(2,1)S(1)}, bf16[288,128]{1,0:T(8,128)(2,1)S(1)}, u32[]{:S(2)}, u32[]{:S(2)}) collective-permute-start(bf16[288,128]{1,0:T(8,128)(2,1)S(1)} %get-tuple-element.27), channel_id=1, source_target_pairs={{0,12},{1,13},{2,14},{3,15},{4,8},{5,9},{6,10},{7,11},{8,4},{9,5},... | collective-permute-start | bytes 221192 | tf_op jit(solution)/shard_map/ppermute | solution.py:573
  48.8 12.9 %slice-start.1 = ((s8[29360128]{0:T(1024)(128)(4,1)}), s8[4194304]{0:T(1024)(128)(4,1)S(1)}, s32[]{:S(2)}) async-start(s8[29360128]{0:T(1024)(128)(4,1)} %bitcast.2), calls=%async_computation.4 | async-start | bytes 8388608
  48.8 12.9 %slice-start.2 = ((s8[29360128]{0:T(1024)(128)(4,1)}), s8[4194304]{0:T(1024)(128)(4,1)S(1)}, s32[]{:S(2)}) async-start(s8[29360128]{0:T(1024)(128)(4,1)} %bitcast.2), calls=%async_computation.5 | async-start | bytes 8388608
  48.8 12.9 %slice-start.3 = ((s8[29360128]{0:T(1024)(128)(4,1)}), s8[4194304]{0:T(1024)(128)(4,1)S(1)}, s32[]{:S(2)}) async-start(s8[29360128]{0:T(1024)(128)(4,1)} %bitcast.2), calls=%async_computation.6 | async-start | bytes 8388608
  48.8 12.9 %slice-start.4 = ((s8[29360128]{0:T(1024)(128)(4,1)}), s8[4194304]{0:T(1024)(128)(4,1)S(1)}, s32[]{:S(2)}) async-start(s8[29360128]{0:T(1024)(128)(4,1)} %bitcast.2), calls=%async_computation.7 | async-start | bytes 8388608
  48.9 12.9 %slice-start.5 = ((s8[29360128]{0:T(1024)(128)(4,1)}), s8[4194304]{0:T(1024)(128)(4,1)S(1)}, s32[]{:S(2)}) async-start(s8[29360128]{0:T(1024)(128)(4,1)} %bitcast.2), calls=%async_computation.8 | async-start | bytes 8388608
  48.9 12.9 %slice-start.6 = ((s8[29360128]{0:T(1024)(128)(4,1)}), s8[4194304]{0:T(1024)(128)(4,1)S(1)}, s32[]{:S(2)}) async-start(s8[29360128]{0:T(1024)(128)(4,1)} %bitcast.2), calls=%async_computation.9 | async-start | bytes 8388608

commit v2 on v1

--- a/solution.py
+++ b/solution.py
@@ -224,12 +224,14 @@
         out[block, NH + per : rows, :] = tail
 
 
-def project_kernel(weight, gathered, gain, out, resid_out, slot_out, pick_out, rows32, lhs, acc, *, slots):
+def project_kernel(weight, here, there, gain, out, resid_out, slot_out, pick_out, rows32, lhs, acc, *, slots):
     batch, width = acc.shape
-    rows = gathered.shape[2]
-    half = lax.axis_index("gx") % 2
+    chips, rows = here.shape[:2]
     place = lax.axis_index("gx")
-    rows32[...] = gathered[...].reshape(batch * rows, HS).astype(jnp.float32)
+    half = place % 2
+    for source, core in ((here, half), (there, 1 - half)):
+        first = pl.multiple_of(core * (chips * rows), 8)
+        rows32[pl.ds(first, chips * rows), :] = source[...].reshape(chips * rows, HS).astype(jnp.float32)
     for head in range(NH):
         lhs[:, head * HS : (head + 1) * HS] = rows32[pl.ds(head, batch, stride=rows), :].astype(jnp.bfloat16)
     acc[...] = jnp.dot(lhs[...], weight[...], preferred_element_type=jnp.float32)
@@ -312,7 +314,21 @@
     work[half : 2 * half, :] = up[:half]
 
 
-def gate_kernel(mine, other, onehot, gate, up, out, gate_out, lhs_out, place_out, tail_out, ring, sems, work, *, slots):
+def both_sides(side, function):
+    for fixed in range(2):
+        pl.when(side == fixed)(functools.partial(function, fixed))
+
+
+def side_sums(blocks, lhs, gate, z, side, slots, work):
+    columns = slice((2 * z + side) * blocks.narrow, (2 * z + side + 1) * blocks.narrow)
+    gates = [
+        jnp.dot(lhs[expert], gate[expert, :, columns], preferred_element_type=jnp.float32) for expert in range(RESIDENT)
+    ]
+    ups = [blocks.times(lhs, z, expert) for expert in range(RESIDENT)]
+    stacked(work, merged(*gates), merged(*ups), RESIDENT * slots)
+
+
+def far_kernel(mine, other, onehot, gate, up, out, lhs_out, place_out, tail_out, ring, sems, work, *, slots):
     batch = mine.shape[0]
     place = lax.axis_index("gx")
     side = place // 2 % 2
@@ -342,34 +358,31 @@
     tail_out[...] = tail
     hot_rows = hot[:, 32 : 32 + place_out.shape[0]]
     place_out[...] = lax.dot_general(hot_rows, eye.astype(jnp.bfloat16), over, preferred_element_type=jnp.float32)
-    narrow = blocks.narrow
-    half = RESIDENT * slots
-
-    for z in range(out.shape[0]):
-        out[z, out.shape[1] - 8 :, :] = tail.astype(jnp.bfloat16)
-        cut = slice(2 * z * narrow, 2 * (z + 1) * narrow)
-        gates = merged(
-            *[jnp.dot(lhs_out[expert], gate[expert, :, cut], preferred_element_type=jnp.float32) for expert in range(RESIDENT)]
-        )
-        lower, upper = gates[:, :narrow], gates[:, narrow:]
-        gate_out[z] = jnp.where(side == 0, lower, upper)
-        ups = [blocks.times(lhs_out, z, expert) for expert in range(RESIDENT)]
-        stacked(work, jnp.where(side == 0, upper, lower), merged(*ups), half)
-        for q in range(narrow // HS):
-            out[z, q * lines : (q + 1) * lines, :] = work[:, q * HS : (q + 1) * HS].astype(jnp.bfloat16)
-
-
-def up_kernel(lhs, tail, gate_sums, up, out, ring, sems, work, *, slots):
+
+    def run(fixed):
+        for z in range(out.shape[0]):
+            out[z, out.shape[1] - 8 :, :] = tail.astype(jnp.bfloat16)
+            side_sums(blocks, lhs_out, gate, z, fixed, slots, work)
+            for q in range(blocks.narrow // HS):
+                value = work[:, q * HS : (q + 1) * HS]
+                out[z, q * lines : (q + 1) * lines, :] = value.astype(jnp.bfloat16)
+
+    both_sides(1 - side, run)
+
+
+def near_kernel(lhs, tail, gate, up, out, ring, sems, work, *, slots):
     side = lax.axis_index("gx") // 2 % 2
     blocks = UpBlocks(up, ring, sems, side)
     lines = 2 * RESIDENT * slots
-    half = RESIDENT * slots
-    for z in range(out.shape[0]):
-        out[z, out.shape[1] - 8 :, :] = tail[...]
-        ups = [blocks.times(lhs, z, expert) for expert in range(RESIDENT)]
-        stacked(work, gate_sums[z], merged(*ups), half)
-        for q in range(blocks.narrow // HS):
-            out[z, q * lines : (q + 1) * lines, :] = work[:, q * HS : (q + 1) * HS]
+
+    def run(fixed):
+        for z in range(out.shape[0]):
+            out[z, out.shape[1] - 8 :, :] = tail[...]
+            side_sums(blocks, lhs, gate, z, fixed, slots, work)
+            for q in range(blocks.narrow // HS):
+                out[z, q * lines : (q + 1) * lines, :] = work[:, q * HS : (q + 1) * HS]
+
+    both_sides(side, run)
 
 
 def pair_kernel(near_sums, got, keep, *sends):
@@ -481,7 +494,6 @@
     lines = 2 * RESIDENT * slots
     bf16, f32 = jnp.bfloat16, jnp.float32
     chips = [[2 * chip + core for chip in range(MSPLIT)] for core in range(2)]
-    cores = [[2 * chip, 2 * chip + 1] for chip in range(MSPLIT)]
     swap = [(i, i ^ 1) for i in range(members)]
     V = pltpu.VMEM
 
@@ -514,12 +526,12 @@
         flops=HINT,
     )
     chip_rows = exchange(sent, chips)
-    gathered = lax.all_gather(chip_rows, "gx", axis=0, tiled=False, axis_index_groups=cores)
+    other_rows = lax.ppermute(chip_rows, "gx", swap)
     mine, resid, onehot, picked = one_block(
         functools.partial(project_kernel, slots=slots),
         [((batch, own_width + HS), bf16), ((batch, own_width), f32), ((batch, HS), f32), ((batch, HS), f32)],
-        (near(out_weight), gathered, norm_gain.reshape(width // HS, HS)),
-        [V, V, V],
+        (near(out_weight), chip_rows, other_rows, norm_gain.reshape(width // HS, HS)),
+        [V, V, V, V],
         "project",
         scratch=[
             pltpu.VMEM((batch * rows, HS), f32),
@@ -542,33 +554,27 @@
             pltpu.VMEM((lines, narrow), f32),
         ]
 
-    far, gate_sums, lhs, place, tail = one_block(
-        functools.partial(gate_kernel, slots=slots),
-        [
-            ((4,) + chunk, bf16),
-            ((4, held, narrow), f32),
-            ((RESIDENT, 16, block_width), bf16),
-            ((held, HS), f32),
-            ((8, HS), f32),
-        ],
+    far, lhs, place, tail = one_block(
+        functools.partial(far_kernel, slots=slots),
+        [((4,) + chunk, bf16), ((RESIDENT, 16, block_width), bf16), ((held, HS), f32), ((8, HS), f32)],
         (near(mine), near(other), near(onehot), near(gate_weight), up_hbm),
         [V, V, V, V, pltpu.HBM],
-        "gate",
+        "far",
         scratch=side_scratch(6),
         grant=7 << 20,
     )
     crossed = lax.ppermute(far, "gx", [(i, i ^ 2) for i in range(members)])
     (near_sums,) = one_block(
-        functools.partial(up_kernel, slots=slots),
+        functools.partial(near_kernel, slots=slots),
         [((4,) + chunk, f32)],
-        (lhs, tail, gate_sums, up_hbm),
+        (lhs, tail, near(gate_weight), up_hbm),
         [V, V, V, pltpu.HBM],
-        "up",
-        scratch=side_scratch(7),
-        grant=8 << 20,
+        "near",
+        scratch=side_scratch(6),
+        grant=7 << 20,
     )
     keep, *sends = one_block(
-        pair_kernel, [(chunk, f32)] + [(chunk, bf16)] * 3, (near_sums, crossed), [V, V], "pair"
+        pair_kernel, [(chunk, f32)] + [(chunk, bf16)] * 3, (near_sums, crossed), [V, V], "pair", flops=HINT // 5
     )
     got = [lax.ppermute(sends[d - 1], "gx", [(i, i ^ 4 * d) for i in range(members)]) for d in (1, 2, 3)]
     (hidden,) = one_block(
@@ -578,7 +584,7 @@
         [V] * 5,
         "gated",
         scratch=[pltpu.VMEM(chunk, f32), pltpu.VMEM(flat, f32)],
-        flops=HINT,
+        flops=HINT // 5,
     )
     hidden_all = exchange(hidden, chips)
     (partial_out,) = one_block(

time: 76.2 us -> 73.2 us (0.961)
  blocking collectives: 38.8 us -> 36.8 us
  Pallas kernels: 23.5 us -> 21.8 us
  waiting for transfers between devices: 7.14 us -> 7.92 us
    all_gather x1 -> x0, blocking collectives: 2.03 us -> none  [fast_on_device(): lax.all_gather(chip_rows, 'gx', axis=0, tiled=False, axis_index_groups=co...]
    pallas_call x8, Pallas kernels: 23.5 us -> 21.8 us  [one_block(): pl.pallas_call(kernel, out_shape=[jax.ShapeDtypeStruct(shape, dtype) for...]
    ppermute x0 -> x1, waiting for transfers between devices: none -> 1.39 us  [fast_on_device(): other_rows = lax.ppermute(chip_rows, 'gx', swap)]
  transfers between devices with their start and end apart: 5 -> 6, of which waited for: 4 -> 5; matrix products, arithmetic and copies ran while one was open for 0% -> 0% of each run, Pallas kernels for 8% -> 9%
where the time goes in v2:
time: 73.2 us; the launch traced here: 73 us
  blocking collectives  36.8 us (50%)
  Pallas kernels  21.8 us (30%)
  waiting for transfers between devices  7.92 us (11%)
  starting transfers between devices  5.63 us (8%)
  between operations  0.78 us (1%)
    all_to_all x3, blocking collectives, exchange(): lax.all_to_all(value, 'gx', split_axis=0, concat_axis=0, tiled=True, axis...  36.8 us
    pallas_call x8, Pallas kernels, one_block(): pl.pallas_call(kernel, out_shape=[jax.ShapeDtypeStruct(shape, dtype) for...  21.8 us
    ppermute x3, starting transfers between devices, fast_on_device(): lax.ppermute(sends[d - 1], 'gx', [(i, i ^ 4 * d) for i in range(members)])  4.45 us
    ppermute x3, waiting for transfers between devices, fast_on_device(): lax.ppermute(sends[d - 1], 'gx', [(i, i ^ 4 * d) for i in range(members)])  4.02 us
  transfers between devices with their start and end apart: 6, of which 5 were waited for; matrix products, arithmetic and copies ran while one was open for 0% of the time, Pallas kernels for 9%

profile of v2, /device:TPU:0, one launch (start us, length us, event | category | flops | bytes accessed | tf_op | source)
XLA Modules:
  0.0 73.0 jit_solution(18006890793416669946)
XLA Ops:
  0.7 0.0 copy-start.1
  0.7 0.0 copy-start.2
  0.7 0.0 copy-start
  0.7 1.9 %attend.1 = bf16[8,80,128]{2,1,0:T(8,128)(2,1)S(1)} custom-call(s32[1]{0:T(128)S(6)} %copy.15.refs_0_, s32[1,2]{1,0:T(1,128)} %refs_1_.1, f32[1,2]{1,0:T(1,128)} %refs_2_.1, bf16[1,8192]{1,0:T(2,128)(2,1)} %refs_3_.1, bf16[1,1024]{1,0:T(2,128)(2,1)} %refs_4_.1, bf16[1,1024]{1,0:T(2,128)(2,1)} %refs_5_.1, bf16[1,8192]{1,0:T(2,128)(2,1)} %refs_6_.1, ...), custom_call_target="tpu_custom_call" | custom-call | flops 99999997952 | bytes 1048576 | tf_op jit(solution)/shard_map/attend/pallas_call | solution.py:148
  2.5 14.9 %all_to_all.15.here = bf16[8,80,128]{2,1,0:T(8,128)(2,1)S(1)} all-to-all(bf16[8,80,128]{2,1,0:T(8,128)(2,1)S(1)} %attend.1), channel_id=1, replica_groups={{0,2,4,6,8,10,12,14},{1,3,5,7,9,11,13,15},{16,18,20,22,24,26,28,30},{17..., dimensions={0} | all-to-all | bytes 327680 | tf_op jit(solution)/shard_map/all_to_all | solution.py:506
  17.4 0.0 collective-permute-start
  17.5 1.4 %collective-permute-done.there = bf16[8,80,128]{2,1,0:T(8,128)(2,1)S(1)} collective-permute-done((bf16[8,80,128]{2,1,0:T(8,128)(2,1)S(1)}, bf16[8,80,128]{2,1,0:T(8,128)(2,1)S(1)}, u32[]{:S(2)}, u32[]{:S(2)}) %collective-permute-start) | collective-permute-done | bytes 163872 | tf_op jit(solution)/shard_map/ppermute | solution.py:529
  18.8 0.0 copy-done.1
  18.8 0.0 copy-done.2
  18.9 1.3 %project.1 = (bf16[16,640]{1,0:T(8,128)(2,1)S(1)}, f32[16,512]{1,0:T(8,128)S(1)}, f32[16,128]{1,0:T(8,128)S(1)}, f32[16,128]{1,0:T(8,128)S(1)}) custom-call(bf16[8192,512]{1,0:T(8,128)(2,1)S(1)} %copy-done.1, bf16[8,80,128]{2,1,0:T(8,128)(2,1)S(1)} %all_to_all.15.here, bf16[8,80,128]{2,1,0:T(8,128)(2,1)S(1)} %collective-permute-done.there, f32[64,128]{1,0:T(8,128)S(1)} %bitcast.3), custom_call_target="tpu_custom_call" | custom-call | bytes 1048576 | tf_op jit(solution)/shard_map/project/pallas_call | solution.py:148
  20.2 0.2 collective-permute-start.1
  20.4 1.0 %collective-permute-done.1.other = bf16[16,640]{1,0:T(8,128)(2,1)S(1)} collective-permute-done((bf16[16,640]{1,0:T(8,128)(2,1)S(1)}, bf16[16,640]{1,0:T(8,128)(2,1)S(1)}, u32[]{:S(2)}, u32[]{:S(2)}) %collective-permute-start.1) | collective-permute-done | bytes 20512 | tf_op jit(solution)/shard_map/ppermute | solution.py:542
  21.4 0.0 copy-done
  21.5 6.7 %far.1 = (bf16[4,288,128]{2,1,0:T(8,128)(2,1)S(1)}, bf16[2,16,1024]{2,1,0:T(8,128)(2,1)S(1)}, f32[24,128]{1,0:T(8,128)S(1)}, f32[8,128]{1,0:T(8,128)S(1)}) custom-call(bf16[16,640]{1,0:T(8,128)(2,1)S(1)} %get-tuple-element.17.mine, bf16[16,640]{1,0:T(8,128)(2,1)S(1)} %collective-permute-done.1.other, f32[16,128]{1,0:T(8,128)S(1)} %get-tuple-element.18.onehot, ...), custom_call_target="tpu_custom_call" | custom-call | bytes 1048576 | tf_op jit(solution)/shard_map/far/pallas_call | solution.py:148
  28.2 1.0 %collective-permute-start.2 = (bf16[4,288,128]{2,1,0:T(8,128)(2,1)S(1)}, bf16[4,288,128]{2,1,0:T(8,128)(2,1)S(1)}, u32[]{:S(2)}, u32[]{:S(2)}) collective-permute-start(bf16[4,288,128]{2,1,0:T(8,128)(2,1)S(1)} %get-tuple-element.21), channel_id=1, source_target_pairs={{0,2},{1,3},{2,0},{3,1},{4,6},{5,7},{6,4},{7,5},{8,10},{9,11},{10,... | collective-permute-start | bytes 884744 | tf_op jit(solution)/shard_map/ppermute | solution.py:566
  29.1 6.7 %near.1.near_sums = f32[4,288,128]{2,1,0:T(8,128)S(1)} custom-call(bf16[2,16,1024]{2,1,0:T(8,128)(2,1)S(1)} %get-tuple-element.19.lhs, f32[8,128]{1,0:T(8,128)S(1)} %get-tuple-element.20.tail, bf16[2,1024,7168]{2,1,0:T(8,128)(2,1)S(1)} %copy-done, bf16[2,1024,7168]{2,1,0:T(8,128)(2,1)} %up.3), custom_call_target="tpu_custom_call" | custom-call | bytes 1048576 | tf_op jit(solution)/shard_map/near/pallas_call | solution.py:148
  35.9 1.5 %collective-permute-done.2.got = bf16[4,288,128]{2,1,0:T(8,128)(2,1)S(1)} collective-permute-done((bf16[4,288,128]{2,1,0:T(8,128)(2,1)S(1)}, bf16[4,288,128]{2,1,0:T(8,128)(2,1)S(1)}, u32[]{:S(2)}, u32[]{:S(2)}) %collective-permute-start.2) | collective-permute-done | bytes 294944 | tf_op jit(solution)/shard_map/ppermute | solution.py:566
  37.3 0.0 slice-start
  37.3 0.0 slice-start.1
  37.3 0.0 slice-start.2
  37.3 0.0 slice-start.3
  37.3 0.1 pair.1
  37.4 0.3 collective-permute-start.3
  37.7 1.0 %collective-permute-start.4 = (bf16[288,128]{1,0:T(8,128)(2,1)S(1)}, bf16[288,128]{1,0:T(8,128)(2,1)S(1)}, u32[]{:S(2)}, u32[]{:S(2)}) collective-permute-start(bf16[288,128]{1,0:T(8,128)(2,1)S(1)} %get-tuple-element.24), channel_id=1, source_target_pairs={{0,8},{1,9},{2,10},{3,11},{4,12},{5,13},{6,14},{7,15},{8,0},{9,1},... | collective-permute-start | bytes 221192 | tf_op jit(solution)/shard_map/ppermute | solution.py:579
  38.7 3.2 %collective-permute-start.5 = (bf16[288,128]{1,0:T(8,128)(2,1)S(1)}, bf16[288,128]{1,0:T(8,128)(2,1)S(1)}, u32[]{:S(2)}, u32[]{:S(2)}) collective-permute-start(bf16[288,128]{1,0:T(8,128)(2,1)S(1)} %get-tuple-element.25), channel_id=1, source_target_pairs={{0,12},{1,13},{2,14},{3,15},{4,8},{5,9},{6,10},{7,11},{8,4},{9,5},... | collective-permute-start | bytes 221192 | tf_op jit(solution)/shard_map/ppermute | solution.py:579
  41.9 0.1 collective-permute-done.3.first
  41.9 3.9 %collective-permute-done.4.second = bf16[288,128]{1,0:T(8,128)(2,1)S(1)} collective-permute-done((bf16[288,128]{1,0:T(8,128)(2,1)S(1)}, bf16[288,128]{1,0:T(8,128)(2,1)S(1)}, u32[]{:S(2)}, u32[]{:S(2)}) %collective-permute-start.4) | collective-permute-done | bytes 73760 | tf_op jit(solution)/shard_map/ppermute | solution.py:579
  45.9 0.0 collective-permute-done.5.third
  45.9 0.0 slice-start.4
  45.9 0.0 slice-start.5
  45.9 0.0 slice-start.6
  45.9 0.2 gated.1
  46.1 12.7 %all_to_all.16.hidden = bf16[8,144,128]{2,1,0:T(8,128)(2,1)S(1)} all-to-all(bf16[8,144,128]{2,1,0:T(8,128)(2,1)S(1)} %gated.1), channel_id=1, replica_groups={{0,2,4,6,8,10,12,14},{1,3,5,7,9,11,13,15},{16,18,20,22,24,26,28,30},{17..., dimensions={0} | all-to-all | bytes 589824 | tf_op jit(solution)/shard_map/all_to_all | solution.py:506
  58.7 0.0 slice-done
  58.7 0.0 slice-done.1
  58.8 0.0 slice-done.2
  58.8 0.0 slice-done.3
  58.8 0.0 slice-done.4
  58.8 0.0 slice-done.5
  58.8 0.0 slice-done.6
  58.8 4.3 %down.2 = bf16[16,8,128]{2,1,0:T(8,128)(2,1)S(1)} custom-call(bf16[8,144,128]{2,1,0:T(8,128)(2,1)S(1)} %all_to_all.16.hidden, bf16[2,7168,1024]{2,1,0:T(8,128)(2,1)S(1)} %bitcast.2, f32[16,128]{1,0:T(8,128)S(1)} %get-tuple-element.27.picked, f32[16,512]{1,0:T(8,128)S(1)} %get-tuple-element.28.resid), custom_call_target="tpu_custom_call" | custom-call | bytes 1048576 | tf_op jit(solution)/shard_map/down/pallas_call | solution.py:148
  63.1 9.2 %all_to_all.17.got = bf16[16,8,128]{2,1,0:T(8,128)(2,1)S(1)} all-to-all(bf16[16,8,128]{2,1,0:T(8,128)(2,1)S(1)} %down.2), channel_id=1, replica_groups=mesh['groups'=2,'gx'=16] {'gx'}, dimensions={0} | all-to-all | bytes 65536 | tf_op jit(solution)/shard_map/all_to_all | solution.py:506
  72.3 0.6 finish.1
  (1 shorter events, 0.0 us)
Async XLA Ops:
  0.7 18.2 %copy-start.1 = (bf16[8192,512]{1,0:T(8,128)(2,1)S(1)}, bf16[8192,512]{1,0:T(8,128)(2,1)}, u32[]{:S(2)}) copy-start(bf16[8192,512]{1,0:T(8,128)(2,1)} %weight.1) | copy-start | bytes 25165828
  0.7 18.2 %copy-start.2 = (f32[8192]{0:T(1024)S(1)}, f32[8192]{0:T(1024)}, u32[]{:S(2)}) copy-start(f32[8192]{0:T(1024)} %param.24) | copy-start | bytes 98308
  0.7 20.8 %copy-start = (bf16[2,1024,7168]{2,1,0:T(8,128)(2,1)S(1)}, bf16[2,1024,7168]{2,1,0:T(8,128)(2,1)}, u32[]{:S(2)}) copy-start(bf16[2,1024,7168]{2,1,0:T(8,128)(2,1)} %gate.3) | copy-start | bytes 88080384
  17.4 1.4 %collective-permute-start = (bf16[8,80,128]{2,1,0:T(8,128)(2,1)S(1)}, bf16[8,80,128]{2,1,0:T(8,128)(2,1)S(1)}, u32[]{:S(2)}, u32[]{:S(2)}) collective-permute-start(bf16[8,80,128]{2,1,0:T(8,128)(2,1)S(1)} %all_to_all.15.here), channel_id=1, source_target_pairs={{0,1},{1,0},{2,3},{3,2},{4,5},{5,4},{6,7},{7,6},{8,9},{9,8},{10,11... | collective-permute-start | bytes 491528 | tf_op jit(solution)/shard_map/ppermute | solution.py:529
  20.2 1.3 %collective-permute-start.1 = (bf16[16,640]{1,0:T(8,128)(2,1)S(1)}, bf16[16,640]{1,0:T(8,128)(2,1)S(1)}, u32[]{:S(2)}, u32[]{:S(2)}) collective-permute-start(bf16[16,640]{1,0:T(8,128)(2,1)S(1)} %get-tuple-element.17.mine), channel_id=1, source_target_pairs={{0,1},{1,0},{2,3},{3,2},{4,5},{5,4},{6,7},{7,6},{8,9},{9,8},{10,11... | collective-permute-start | bytes 61448 | tf_op jit(solution)/shard_map/ppermute | solution.py:542
  28.2 9.1 %collective-permute-start.2 = (bf16[4,288,128]{2,1,0:T(8,128)(2,1)S(1)}, bf16[4,288,128]{2,1,0:T(8,128)(2,1)S(1)}, u32[]{:S(2)}, u32[]{:S(2)}) collective-permute-start(bf16[4,288,128]{2,1,0:T(8,128)(2,1)S(1)} %get-tuple-element.21), channel_id=1, source_target_pairs={{0,2},{1,3},{2,0},{3,1},{4,6},{5,7},{6,4},{7,5},{8,10},{9,11},{10,... | collective-permute-start | bytes 884744 | tf_op jit(solution)/shard_map/ppermute | solution.py:566
  37.3 21.4 %slice-start = ((s8[29360128]{0:T(1024)(128)(4,1)}), s8[4194304]{0:T(1024)(128)(4,1)S(1)}, s32[]{:S(2)}) async-start(s8[29360128]{0:T(1024)(128)(4,1)} %bitcast.1), calls=%async_computation.3 | async-start | bytes 8388608
  37.3 21.4 %slice-start.1 = ((s8[29360128]{0:T(1024)(128)(4,1)}), s8[4194304]{0:T(1024)(128)(4,1)S(1)}, s32[]{:S(2)}) async-start(s8[29360128]{0:T(1024)(128)(4,1)} %bitcast.1), calls=%async_computation.4 | async-start | bytes 8388608
  37.3 21.4 %slice-start.2 = ((s8[29360128]{0:T(1024)(128)(4,1)}), s8[4194304]{0:T(1024)(128)(4,1)S(1)}, s32[]{:S(2)}) async-start(s8[29360128]{0:T(1024)(128)(4,1)} %bitcast.1), calls=%async_computation.5 | async-start | bytes 8388608
  37.3 21.4 %slice-start.3 = ((s8[29360128]{0:T(1024)(128)(4,1)}), s8[4194304]{0:T(1024)(128)(4,1)S(1)}, s32[]{:S(2)}) async-start(s8[29360128]{0:T(1024)(128)(4,1)} %bitcast.1), calls=%async_computation.6 | async-start | bytes 8388608
  37.4 4.5 %collective-permute-start.3 = (bf16[288,128]{1,0:T(8,128)(2,1)S(1)}, bf16[288,128]{1,0:T(8,128)(2,1)S(1)}, u32[]{:S(2)}, u32[]{:S(2)}) collective-permute-start(bf16[288,128]{1,0:T(8,128)(2,1)S(1)} %get-tuple-element.23), channel_id=1, source_target_pairs={{0,4},{1,5},{2,6},{3,7},{4,0},{5,1},{6,2},{7,3},{8,12},{9,13},{10,... | collective-permute-start | bytes 221192 | tf_op jit(solution)/shard_map/ppermute | solution.py:579
  37.7 8.2 %collective-permute-start.4 = (bf16[288,128]{1,0:T(8,128)(2,1)S(1)}, bf16[288,128]{1,0:T(8,128)(2,1)S(1)}, u32[]{:S(2)}, u32[]{:S(2)}) collective-permute-start(bf16[288,128]{1,0:T(8,128)(2,1)S(1)} %get-tuple-element.24), channel_id=1, source_target_pairs={{0,8},{1,9},{2,10},{3,11},{4,12},{5,13},{6,14},{7,15},{8,0},{9,1},... | collective-permute-start | bytes 221192 | tf_op jit(solution)/shard_map/ppermute | solution.py:579
  38.7 7.2 %collective-permute-start.5 = (bf16[288,128]{1,0:T(8,128)(2,1)S(1)}, bf16[288,128]{1,0:T(8,128)(2,1)S(1)}, u32[]{:S(2)}, u32[]{:S(2)}) collective-permute-start(bf16[288,128]{1,0:T(8,128)(2,1)S(1)} %get-tuple-element.25), channel_id=1, source_target_pairs={{0,12},{1,13},{2,14},{3,15},{4,8},{5,9},{6,10},{7,11},{8,4},{9,5},... | collective-permute-start | bytes 221192 | tf_op jit(solution)/shard_map/ppermute | solution.py:579
  45.9 12.9 %slice-start.4 = ((s8[29360128]{0:T(1024)(128)(4,1)}), s8[4194304]{0:T(1024)(128)(4,1)S(1)}, s32[]{:S(2)}) async-start(s8[29360128]{0:T(1024)(128)(4,1)} %bitcast.1), calls=%async_computation.7 | async-start | bytes 8388608
  45.9 12.9 %slice-start.5 = ((s8[29360128]{0:T(1024)(128)(4,1)}), s8[4194304]{0:T(1024)(128)(4,1)S(1)}, s32[]{:S(2)}) async-start(s8[29360128]{0:T(1024)(128)(4,1)} %bitcast.1), calls=%async_computation.8 | async-start | bytes 8388608
  45.9 12.9 %slice-start.6 = ((s8[29360128]{0:T(1024)(128)(4,1)}), s8[4194304]{0:T(1024)(128)(4,1)S(1)}, s32[]{:S(2)}) async-start(s8[29360128]{0:T(1024)(128)(4,1)} %bitcast.1), calls=%async_computation.9 | async-start | bytes 8388608

commit v3 on v2

--- a/solution.py
+++ b/solution.py
@@ -394,7 +394,6 @@
 
 def gated_kernel(keep, first, second, third, place, out, work, packed, *, slots, width):
     lines = 2 * RESIDENT * slots
-    blocks = out.shape[0]
     per = (keep.shape[0] - 8) // lines
     total = keep[...]
     for got in (first, second, third):
@@ -410,34 +409,47 @@
         gate = work[q * lines : q * lines + half, :] * scale
         up = work[q * lines + half : (q + 1) * lines, :] * scale
         packed[q * half : (q + 1) * half, :] = gate / (1.0 + jnp.exp(-gate)) * up
-    hidden = packed[...].astype(jnp.bfloat16)
-    for block in range(blocks):
-        out[block] = hidden
-
-
-def down_kernel(hidden, down, picked, resid, out, spread, rows32, lhs, acc, *, slots):
-    blocks = hidden.shape[0]
-    half = lax.axis_index("gx") % 2
+    out[...] = packed[...].astype(jnp.bfloat16)
+
+
+def gather_kernel(own, first, second, third, out):
+    for d, value in enumerate((own, first, second, third)):
+        out[d] = value[...]
+
+
+def down_side(hidden, down, side, rows32, lhs, acc, slots):
+    own = lax.axis_index("gx") // 4
     each = RESIDENT * slots
-    per = lhs.shape[2] // blocks // HS
-    for block in range(blocks):
-        rows32[block] = hidden[block].astype(jnp.float32)
-        for q in range(per):
-            at = (block * per + q) * HS
+    narrow = lhs.shape[3]
+    for z in range(4):
+        rows32[z] = hidden[z ^ own].astype(jnp.float32)
+        for q in range(narrow // HS):
             for expert in range(RESIDENT):
                 start = q * each + expert * slots // 8 * 8
-                lhs[expert, :, at : at + HS] = rows32[block, start : start + 16, :].astype(jnp.bfloat16)
-    tile = acc.shape[1] // 2
-
-    def columns(k, carry):
-        cut = pl.ds(pl.multiple_of(k * tile, tile), tile)
+                piece = rows32[z, start : start + 16, :]
+                lhs[z, expert, :, q * HS : (q + 1) * HS] = piece.astype(jnp.bfloat16)
+
+    def run(fixed):
         for expert in range(RESIDENT):
-            acc[expert * 16 : (expert + 1) * 16, cut] = jnp.dot(
-                lhs[expert], down[expert, :, cut], preferred_element_type=jnp.float32
-            )
-        return carry
-
-    lax.fori_loop(0, 2, columns, 0)
+            total = None
+            for z in range(4):
+                cut = slice((2 * z + fixed) * narrow, (2 * z + fixed + 1) * narrow)
+                term = jnp.dot(lhs[z, expert], down[expert, cut, :], preferred_element_type=jnp.float32)
+                total = term if total is None else total + term
+            acc[expert * 16 : (expert + 1) * 16, :] = total
+
+    both_sides(side, run)
+
+
+def down_near_kernel(hidden, down, acc, rows32, lhs, *, slots):
+    down_side(hidden, down, lax.axis_index("gx") // 2 % 2, rows32, lhs, acc, slots)
+
+
+def down_far_kernel(hidden, down, near_acc, picked, resid, out, spread, rows32, lhs, acc, *, slots):
+    down_side(hidden, down, 1 - lax.axis_index("gx") // 2 % 2, rows32, lhs, acc, slots)
+    half = lax.axis_index("gx") % 2
+    blocks = 8
+    acc[...] = acc[...] + near_acc[...]
     weight = picked[...].astype(jnp.bfloat16)[:, : RESIDENT * 16]
     result = None
     for part in split_three(acc[...]):
@@ -466,6 +478,9 @@
         for q in range(per):
             at = (block * per + q) * HS
             out[0:1, at : at + HS] = total[q : q + 1, :].astype(jnp.bfloat16)
+
+
+HG = 0
 
 
 def fast_on_device(
@@ -579,26 +594,33 @@
     got = [lax.ppermute(sends[d - 1], "gx", [(i, i ^ 4 * d) for i in range(members)]) for d in (1, 2, 3)]
     (hidden,) = one_block(
         functools.partial(gated_kernel, slots=slots, width=width),
-        [((MSPLIT,) + flat, bf16)],
+        [(flat, bf16)],
         (keep, *got, place),
         [V] * 5,
         "gated",
         scratch=[pltpu.VMEM(chunk, f32), pltpu.VMEM(flat, f32)],
         flops=HINT // 5,
     )
-    hidden_all = exchange(hidden, chips)
+    parts = [lax.ppermute(hidden, "gx", [(i, i ^ 4 * d) for i in range(members)]) for d in (1, 2, 3)]
+    (near_hidden,) = one_block(gather_kernel, [((4,) + flat, bf16)], (hidden, *parts), [V] * 4, "gather", flops=HG)
+    far_hidden = lax.ppermute(near_hidden, "gx", [(i, i ^ 2) for i in range(members)])
+    side_rows = [pltpu.VMEM((4,) + flat, f32), pltpu.VMEM((4, RESIDENT, 16, narrow), bf16)]
+    sums = (RESIDENT * 16, block_width)
+    (near_acc,) = one_block(
+        functools.partial(down_near_kernel, slots=slots),
+        [(sums, f32)],
+        (near_hidden, near(down_weight)),
+        [V, V],
+        "down_near",
+        scratch=side_rows,
+    )
     (partial_out,) = one_block(
-        functools.partial(down_kernel, slots=slots),
+        functools.partial(down_far_kernel, slots=slots),
         [((members, block_width // HS, HS), bf16)],
-        (hidden_all, near(down_weight), picked, resid),
-        [V, V, V, V],
-        "down",
-        scratch=[
-            pltpu.VMEM((members * block_width // HS, HS), f32),
-            pltpu.VMEM((MSPLIT,) + flat, f32),
-            pltpu.VMEM((RESIDENT, 16, hidden_cols), bf16),
-            pltpu.VMEM((RESIDENT * 16, block_width), f32),
-        ],
+        (far_hidden, near(down_weight), near_acc, picked, resid),
+        [V] * 5,
+        "down_far",
+        scratch=[pltpu.VMEM((members * block_width // HS, HS), f32)] + side_rows + [pltpu.VMEM(sums, f32)],
     )
     last = exchange(partial_out, None)
     (out,) = one_block(finish_kernel, [((1, width), bf16)], (last,), [V], "finish")

time: 73.2 us -> 71.7 us (0.980)
  blocking collectives: 36.8 us -> 25 us
  starting transfers between devices: 5.63 us -> 11.1 us
  waiting for transfers between devices: 7.92 us -> 12.6 us
    all_to_all x3 -> x2, blocking collectives: 36.8 us -> 25 us  [exchange(): lax.all_to_all(value, 'gx', split_axis=0, concat_axis=0, tiled=True, axis...]
    ppermute x0 -> x4, starting transfers between devices: none -> 5.5 us  [the longest x3 4.45 us: fast_on_device(): lax.ppermute(hidden, 'gx', [(i, i ^ 4 * d) for i in range(members)])]
    ppermute x0 -> x4, waiting for transfers between devices: none -> 4.69 us  [the longest x3 2.77 us: fast_on_device(): lax.ppermute(hidden, 'gx', [(i, i ^ 4 * d) for i in range(members)])]
    pallas_call x8 -> x10, Pallas kernels: 21.8 us -> 21.9 us  [one_block(): pl.pallas_call(kernel, out_shape=[jax.ShapeDtypeStruct(shape, dtype) for...]
  transfers between devices with their start and end apart: 6 -> 10, of which waited for: 5 -> 8; matrix products, arithmetic and copies ran while one was open for 0% -> 0% of each run, Pallas kernels for 9% -> 12%
where the time goes in v3:
time: 71.7 us; the launch traced here: 71.5 us
  blocking collectives  25 us (35%)
  Pallas kernels  21.9 us (31%)
  waiting for transfers between devices  12.6 us (18%)
  starting transfers between devices  11.1 us (15%)
  between operations  0.79 us (1%)
    all_to_all x2, blocking collectives, exchange(): lax.all_to_all(value, 'gx', split_axis=0, concat_axis=0, tiled=True, axis...  25 us
    pallas_call x10, Pallas kernels, one_block(): pl.pallas_call(kernel, out_shape=[jax.ShapeDtypeStruct(shape, dtype) for...  21.9 us
    ppermute x3, starting transfers between devices, fast_on_device(): lax.ppermute(hidden, 'gx', [(i, i ^ 4 * d) for i in range(members)])  4.45 us
    ppermute x3, starting transfers between devices, fast_on_device(): lax.ppermute(sends[d - 1], 'gx', [(i, i ^ 4 * d) for i in range(members)])  4.45 us
    ppermute x3, waiting for transfers between devices, fast_on_device(): lax.ppermute(sends[d - 1], 'gx', [(i, i ^ 4 * d) for i in range(members)])  4.02 us
    ppermute x3, waiting for transfers between devices, fast_on_device(): lax.ppermute(hidden, 'gx', [(i, i ^ 4 * d) for i in range(members)])  2.77 us
    ppermute x1, waiting for transfers between devices, fast_on_device(): lax.ppermute(near_hidden, 'gx', [(i, i ^ 2) for i in range(members)])  1.92 us
    ppermute x1, waiting for transfers between devices, fast_on_device(): crossed = lax.ppermute(far, 'gx', [(i, i ^ 2) for i in range(members)])  1.45 us
  transfers between devices with their start and end apart: 10, of which 8 were waited for; matrix products, arithmetic and copies ran while one was open for 0% of the time, Pallas kernels for 12%

profile of v3, /device:TPU:0, one launch (start us, length us, event | category | flops | bytes accessed | tf_op | source)
XLA Modules:
  0.0 71.5 jit_solution(13196771235683423420)
XLA Ops:
  0.7 0.0 copy-start.1
  0.7 0.0 copy-start.2
  0.7 0.0 copy-start
  0.7 1.9 %attend.1 = bf16[8,80,128]{2,1,0:T(8,128)(2,1)S(1)} custom-call(s32[1]{0:T(128)S(6)} %copy.15.refs_0_, s32[1,2]{1,0:T(1,128)} %refs_1_.1, f32[1,2]{1,0:T(1,128)} %refs_2_.1, bf16[1,8192]{1,0:T(2,128)(2,1)} %refs_3_.1, bf16[1,1024]{1,0:T(2,128)(2,1)} %refs_4_.1, bf16[1,1024]{1,0:T(2,128)(2,1)} %refs_5_.1, bf16[1,8192]{1,0:T(2,128)(2,1)} %refs_6_.1, ...), custom_call_target="tpu_custom_call" | custom-call | flops 99999997952 | bytes 1048576 | tf_op jit(solution)/shard_map/attend/pallas_call | solution.py:148
  2.5 14.9 %all_to_all.10.here = bf16[8,80,128]{2,1,0:T(8,128)(2,1)S(1)} all-to-all(bf16[8,80,128]{2,1,0:T(8,128)(2,1)S(1)} %attend.1), channel_id=1, replica_groups={{0,2,4,6,8,10,12,14},{1,3,5,7,9,11,13,15},{16,18,20,22,24,26,28,30},{17..., dimensions={0} | all-to-all | bytes 327680 | tf_op jit(solution)/shard_map/all_to_all | solution.py:521
  17.4 0.0 collective-permute-start
  17.5 1.4 %collective-permute-done.there = bf16[8,80,128]{2,1,0:T(8,128)(2,1)S(1)} collective-permute-done((bf16[8,80,128]{2,1,0:T(8,128)(2,1)S(1)}, bf16[8,80,128]{2,1,0:T(8,128)(2,1)S(1)}, u32[]{:S(2)}, u32[]{:S(2)}) %collective-permute-start) | collective-permute-done | bytes 163872 | tf_op jit(solution)/shard_map/ppermute | solution.py:544
  18.8 0.0 copy-done.1
  18.8 0.0 copy-done.2
  18.9 1.3 %project.1 = (bf16[16,640]{1,0:T(8,128)(2,1)S(1)}, f32[16,512]{1,0:T(8,128)S(1)}, f32[16,128]{1,0:T(8,128)S(1)}, f32[16,128]{1,0:T(8,128)S(1)}) custom-call(bf16[8192,512]{1,0:T(8,128)(2,1)S(1)} %copy-done.1, bf16[8,80,128]{2,1,0:T(8,128)(2,1)S(1)} %all_to_all.10.here, bf16[8,80,128]{2,1,0:T(8,128)(2,1)S(1)} %collective-permute-done.there, f32[64,128]{1,0:T(8,128)S(1)} %bitcast.3), custom_call_target="tpu_custom_call" | custom-call | bytes 1048576 | tf_op jit(solution)/shard_map/project/pallas_call | solution.py:148
  20.2 0.2 collective-permute-start.1
  20.4 1.0 %collective-permute-done.1.other = bf16[16,640]{1,0:T(8,128)(2,1)S(1)} collective-permute-done((bf16[16,640]{1,0:T(8,128)(2,1)S(1)}, bf16[16,640]{1,0:T(8,128)(2,1)S(1)}, u32[]{:S(2)}, u32[]{:S(2)}) %collective-permute-start.1) | collective-permute-done | bytes 20512 | tf_op jit(solution)/shard_map/ppermute | solution.py:557
  21.4 0.0 copy-done
  21.5 6.7 %far.1 = (bf16[4,288,128]{2,1,0:T(8,128)(2,1)S(1)}, bf16[2,16,1024]{2,1,0:T(8,128)(2,1)S(1)}, f32[24,128]{1,0:T(8,128)S(1)}, f32[8,128]{1,0:T(8,128)S(1)}) custom-call(bf16[16,640]{1,0:T(8,128)(2,1)S(1)} %get-tuple-element.17.mine, bf16[16,640]{1,0:T(8,128)(2,1)S(1)} %collective-permute-done.1.other, f32[16,128]{1,0:T(8,128)S(1)} %get-tuple-element.18.onehot, ...), custom_call_target="tpu_custom_call" | custom-call | bytes 1048576 | tf_op jit(solution)/shard_map/far/pallas_call | solution.py:148
  28.2 1.0 %collective-permute-start.2 = (bf16[4,288,128]{2,1,0:T(8,128)(2,1)S(1)}, bf16[4,288,128]{2,1,0:T(8,128)(2,1)S(1)}, u32[]{:S(2)}, u32[]{:S(2)}) collective-permute-start(bf16[4,288,128]{2,1,0:T(8,128)(2,1)S(1)} %get-tuple-element.21), channel_id=1, source_target_pairs={{0,2},{1,3},{2,0},{3,1},{4,6},{5,7},{6,4},{7,5},{8,10},{9,11},{10,... | collective-permute-start | bytes 884744 | tf_op jit(solution)/shard_map/ppermute | solution.py:581
  29.1 6.7 %near.1.near_sums = f32[4,288,128]{2,1,0:T(8,128)S(1)} custom-call(bf16[2,16,1024]{2,1,0:T(8,128)(2,1)S(1)} %get-tuple-element.19.lhs, f32[8,128]{1,0:T(8,128)S(1)} %get-tuple-element.20.tail, bf16[2,1024,7168]{2,1,0:T(8,128)(2,1)S(1)} %copy-done, bf16[2,1024,7168]{2,1,0:T(8,128)(2,1)} %up.3), custom_call_target="tpu_custom_call" | custom-call | bytes 1048576 | tf_op jit(solution)/shard_map/near/pallas_call | solution.py:148
  35.9 1.5 %collective-permute-done.2.got = bf16[4,288,128]{2,1,0:T(8,128)(2,1)S(1)} collective-permute-done((bf16[4,288,128]{2,1,0:T(8,128)(2,1)S(1)}, bf16[4,288,128]{2,1,0:T(8,128)(2,1)S(1)}, u32[]{:S(2)}, u32[]{:S(2)}) %collective-permute-start.2) | collective-permute-done | bytes 294944 | tf_op jit(solution)/shard_map/ppermute | solution.py:581
  37.3 0.0 slice-start
  37.3 0.0 slice-start.1
  37.3 0.0 slice-start.2
  37.3 0.0 slice-start.3
  37.3 0.1 pair.1
  37.4 0.3 collective-permute-start.3
  37.7 1.0 %collective-permute-start.4 = (bf16[288,128]{1,0:T(8,128)(2,1)S(1)}, bf16[288,128]{1,0:T(8,128)(2,1)S(1)}, u32[]{:S(2)}, u32[]{:S(2)}) collective-permute-start(bf16[288,128]{1,0:T(8,128)(2,1)S(1)} %get-tuple-element.24), channel_id=1, source_target_pairs={{0,8},{1,9},{2,10},{3,11},{4,12},{5,13},{6,14},{7,15},{8,0},{9,1},... | collective-permute-start | bytes 221192 | tf_op jit(solution)/shard_map/ppermute | solution.py:594
  38.7 3.2 %collective-permute-start.5 = (bf16[288,128]{1,0:T(8,128)(2,1)S(1)}, bf16[288,128]{1,0:T(8,128)(2,1)S(1)}, u32[]{:S(2)}, u32[]{:S(2)}) collective-permute-start(bf16[288,128]{1,0:T(8,128)(2,1)S(1)} %get-tuple-element.25), channel_id=1, source_target_pairs={{0,12},{1,13},{2,14},{3,15},{4,8},{5,9},{6,10},{7,11},{8,4},{9,5},... | collective-permute-start | bytes 221192 | tf_op jit(solution)/shard_map/ppermute | solution.py:594
  41.9 0.1 collective-permute-done.3.first
  41.9 3.9 %collective-permute-done.4.second = bf16[288,128]{1,0:T(8,128)(2,1)S(1)} collective-permute-done((bf16[288,128]{1,0:T(8,128)(2,1)S(1)}, bf16[288,128]{1,0:T(8,128)(2,1)S(1)}, u32[]{:S(2)}, u32[]{:S(2)}) %collective-permute-start.4) | collective-permute-done | bytes 73760 | tf_op jit(solution)/shard_map/ppermute | solution.py:594
  45.9 0.0 collective-permute-done.5.third
  45.9 0.1 gated.1.own
  46.0 2.3 %collective-permute-start.8 = (bf16[144,128]{1,0:T(8,128)(2,1)S(1)}, bf16[144,128]{1,0:T(8,128)(2,1)S(1)}, u32[]{:S(2)}, u32[]{:S(2)}) collective-permute-start(bf16[144,128]{1,0:T(8,128)(2,1)S(1)} %gated.1.own), channel_id=1, source_target_pairs={{0,12},{1,13},{2,14},{3,15},{4,8},{5,9},{6,10},{7,11},{8,4},{9,5},... | collective-permute-start | bytes 110600 | tf_op jit(solution)/shard_map/ppermute | solution.py:604
  48.3 0.6 collective-permute-start.7
  48.9 1.6 %collective-permute-start.6 = (bf16[144,128]{1,0:T(8,128)(2,1)S(1)}, bf16[144,128]{1,0:T(8,128)(2,1)S(1)}, u32[]{:S(2)}, u32[]{:S(2)}) collective-permute-start(bf16[144,128]{1,0:T(8,128)(2,1)S(1)} %gated.1.own), channel_id=1, source_target_pairs={{0,4},{1,5},{2,6},{3,7},{4,0},{5,1},{6,2},{7,3},{8,12},{9,13},{10,... | collective-permute-start | bytes 110600 | tf_op jit(solution)/shard_map/ppermute | solution.py:604
  50.5 1.4 %collective-permute-done.8.third = bf16[144,128]{1,0:T(8,128)(2,1)S(1)} collective-permute-done((bf16[144,128]{1,0:T(8,128)(2,1)S(1)}, bf16[144,128]{1,0:T(8,128)(2,1)S(1)}, u32[]{:S(2)}, u32[]{:S(2)}) %collective-permute-start.8) | collective-permute-done | bytes 36896 | tf_op jit(solution)/shard_map/ppermute | solution.py:604
  51.9 1.4 %collective-permute-done.7.second = bf16[144,128]{1,0:T(8,128)(2,1)S(1)} collective-permute-done((bf16[144,128]{1,0:T(8,128)(2,1)S(1)}, bf16[144,128]{1,0:T(8,128)(2,1)S(1)}, u32[]{:S(2)}, u32[]{:S(2)}) %collective-permute-start.7) | collective-permute-done | bytes 36896 | tf_op jit(solution)/shard_map/ppermute | solution.py:604
  53.3 0.0 collective-permute-done.6.first
  53.3 1.1 %collective-permute-start.9 = (bf16[4,144,128]{2,1,0:T(8,128)(2,1)S(1)}, bf16[4,144,128]{2,1,0:T(8,128)(2,1)S(1)}, u32[]{:S(2)}, u32[]{:S(2)}) collective-permute-start(bf16[4,144,128]{2,1,0:T(8,128)(2,1)S(1)} %gather.1.hidden), channel_id=1, source_target_pairs={{0,2},{1,3},{2,0},{3,1},{4,6},{5,7},{6,4},{7,5},{8,10},{9,11},{10,... | collective-permute-start | bytes 442376 | tf_op jit(solution)/shard_map/ppermute | solution.py:606
  54.3 0.0 slice-done
  54.3 0.0 slice-done.1
  54.3 0.0 slice-done.2
  54.3 0.0 slice-done.3
  54.4 0.0 slice-done.4
  54.4 0.0 slice-done.5
  54.4 0.0 slice-done.6
  54.4 2.2 %down_near.1.near_acc = f32[32,1024]{1,0:T(8,128)S(1)} custom-call(bf16[4,144,128]{2,1,0:T(8,128)(2,1)S(1)} %gather.1.hidden, bf16[2,7168,1024]{2,1,0:T(8,128)(2,1)S(1)} %bitcast.2), custom_call_target="tpu_custom_call" | custom-call | bytes 1048576 | tf_op jit(solution)/shard_map/down_near/pallas_call | solution.py:148
  56.6 1.9 %collective-permute-done.9.hidden = bf16[4,144,128]{2,1,0:T(8,128)(2,1)S(1)} collective-permute-done((bf16[4,144,128]{2,1,0:T(8,128)(2,1)S(1)}, bf16[4,144,128]{2,1,0:T(8,128)(2,1)S(1)}, u32[]{:S(2)}, u32[]{:S(2)}) %collective-permute-start.9) | collective-permute-done | bytes 147488 | tf_op jit(solution)/shard_map/ppermute | solution.py:606
  58.5 2.3 %down_far.1 = bf16[16,8,128]{2,1,0:T(8,128)(2,1)S(1)} custom-call(bf16[4,144,128]{2,1,0:T(8,128)(2,1)S(1)} %collective-permute-done.9.hidden, bf16[2,7168,1024]{2,1,0:T(8,128)(2,1)S(1)} %bitcast.2, f32[32,1024]{1,0:T(8,128)S(1)} %down_near.1.near_acc, f32[16,128]{1,0:T(8,128)S(1)} %get-tuple-element.27.picked, f32[16,512]{1,0:T(8,128)S(1)} %get-tuple-element.28.resid), custom_call_target="tpu_custom_call" | custom-call | bytes 1048576 | tf_op jit(solution)/shard_map/down_far/pallas_call | solution.py:148
  60.8 10.1 %all_to_all.11.got = bf16[16,8,128]{2,1,0:T(8,128)(2,1)S(1)} all-to-all(bf16[16,8,128]{2,1,0:T(8,128)(2,1)S(1)} %down_far.1), channel_id=1, replica_groups=mesh['groups'=2,'gx'=16] {'gx'}, dimensions={0} | all-to-all | bytes 65536 | tf_op jit(solution)/shard_map/all_to_all | solution.py:521
  70.8 0.6 finish.1
  (5 shorter events, 0.0 us)
Async XLA Ops:
  0.7 18.2 %copy-start.1 = (bf16[8192,512]{1,0:T(8,128)(2,1)S(1)}, bf16[8192,512]{1,0:T(8,128)(2,1)}, u32[]{:S(2)}) copy-start(bf16[8192,512]{1,0:T(8,128)(2,1)} %weight.1) | copy-start | bytes 25165828
  0.7 18.2 %copy-start.2 = (f32[8192]{0:T(1024)S(1)}, f32[8192]{0:T(1024)}, u32[]{:S(2)}) copy-start(f32[8192]{0:T(1024)} %param.24) | copy-start | bytes 98308
  0.7 20.8 %copy-start = (bf16[2,1024,7168]{2,1,0:T(8,128)(2,1)S(1)}, bf16[2,1024,7168]{2,1,0:T(8,128)(2,1)}, u32[]{:S(2)}) copy-start(bf16[2,1024,7168]{2,1,0:T(8,128)(2,1)} %gate.3) | copy-start | bytes 88080384
  17.4 1.4 %collective-permute-start = (bf16[8,80,128]{2,1,0:T(8,128)(2,1)S(1)}, bf16[8,80,128]{2,1,0:T(8,128)(2,1)S(1)}, u32[]{:S(2)}, u32[]{:S(2)}) collective-permute-start(bf16[8,80,128]{2,1,0:T(8,128)(2,1)S(1)} %all_to_all.10.here), channel_id=1, source_target_pairs={{0,1},{1,0},{2,3},{3,2},{4,5},{5,4},{6,7},{7,6},{8,9},{9,8},{10,11... | collective-permute-start | bytes 491528 | tf_op jit(solution)/shard_map/ppermute | solution.py:544
  20.2 1.3 %collective-permute-start.1 = (bf16[16,640]{1,0:T(8,128)(2,1)S(1)}, bf16[16,640]{1,0:T(8,128)(2,1)S(1)}, u32[]{:S(2)}, u32[]{:S(2)}) collective-permute-start(bf16[16,640]{1,0:T(8,128)(2,1)S(1)} %get-tuple-element.17.mine), channel_id=1, source_target_pairs={{0,1},{1,0},{2,3},{3,2},{4,5},{5,4},{6,7},{7,6},{8,9},{9,8},{10,11... | collective-permute-start | bytes 61448 | tf_op jit(solution)/shard_map/ppermute | solution.py:557
  28.2 9.1 %collective-permute-start.2 = (bf16[4,288,128]{2,1,0:T(8,128)(2,1)S(1)}, bf16[4,288,128]{2,1,0:T(8,128)(2,1)S(1)}, u32[]{:S(2)}, u32[]{:S(2)}) collective-permute-start(bf16[4,288,128]{2,1,0:T(8,128)(2,1)S(1)} %get-tuple-element.21), channel_id=1, source_target_pairs={{0,2},{1,3},{2,0},{3,1},{4,6},{5,7},{6,4},{7,5},{8,10},{9,11},{10,... | collective-permute-start | bytes 884744 | tf_op jit(solution)/shard_map/ppermute | solution.py:581
  37.3 17.0 %slice-start = ((s8[29360128]{0:T(1024)(128)(4,1)}), s8[4194304]{0:T(1024)(128)(4,1)S(1)}, s32[]{:S(2)}) async-start(s8[29360128]{0:T(1024)(128)(4,1)} %bitcast.1), calls=%async_computation.2 | async-start | bytes 8388608
  37.3 17.0 %slice-start.1 = ((s8[29360128]{0:T(1024)(128)(4,1)}), s8[4194304]{0:T(1024)(128)(4,1)S(1)}, s32[]{:S(2)}) async-start(s8[29360128]{0:T(1024)(128)(4,1)} %bitcast.1), calls=%async_computation.3 | async-start | bytes 8388608
  37.3 17.0 %slice-start.2 = ((s8[29360128]{0:T(1024)(128)(4,1)}), s8[4194304]{0:T(1024)(128)(4,1)S(1)}, s32[]{:S(2)}) async-start(s8[29360128]{0:T(1024)(128)(4,1)} %bitcast.1), calls=%async_computation.4 | async-start | bytes 8388608
  37.3 17.0 %slice-start.3 = ((s8[29360128]{0:T(1024)(128)(4,1)}), s8[4194304]{0:T(1024)(128)(4,1)S(1)}, s32[]{:S(2)}) async-start(s8[29360128]{0:T(1024)(128)(4,1)} %bitcast.1), calls=%async_computation.5 | async-start | bytes 8388608
  37.4 4.5 %collective-permute-start.3 = (bf16[288,128]{1,0:T(8,128)(2,1)S(1)}, bf16[288,128]{1,0:T(8,128)(2,1)S(1)}, u32[]{:S(2)}, u32[]{:S(2)}) collective-permute-start(bf16[288,128]{1,0:T(8,128)(2,1)S(1)} %get-tuple-element.23), channel_id=1, source_target_pairs={{0,4},{1,5},{2,6},{3,7},{4,0},{5,1},{6,2},{7,3},{8,12},{9,13},{10,... | collective-permute-start | bytes 221192 | tf_op jit(solution)/shard_map/ppermute | solution.py:594
  37.7 8.2 %collective-permute-start.4 = (bf16[288,128]{1,0:T(8,128)(2,1)S(1)}, bf16[288,128]{1,0:T(8,128)(2,1)S(1)}, u32[]{:S(2)}, u32[]{:S(2)}) collective-permute-start(bf16[288,128]{1,0:T(8,128)(2,1)S(1)} %get-tuple-element.24), channel_id=1, source_target_pairs={{0,8},{1,9},{2,10},{3,11},{4,12},{5,13},{6,14},{7,15},{8,0},{9,1},... | collective-permute-start | bytes 221192 | tf_op jit(solution)/shard_map/ppermute | solution.py:594
  38.7 7.2 %collective-permute-start.5 = (bf16[288,128]{1,0:T(8,128)(2,1)S(1)}, bf16[288,128]{1,0:T(8,128)(2,1)S(1)}, u32[]{:S(2)}, u32[]{:S(2)}) collective-permute-start(bf16[288,128]{1,0:T(8,128)(2,1)S(1)} %get-tuple-element.25), channel_id=1, source_target_pairs={{0,12},{1,13},{2,14},{3,15},{4,8},{5,9},{6,10},{7,11},{8,4},{9,5},... | collective-permute-start | bytes 221192 | tf_op jit(solution)/shard_map/ppermute | solution.py:594
  45.9 8.5 %slice-start.4 = ((s8[29360128]{0:T(1024)(128)(4,1)}), s8[4194304]{0:T(1024)(128)(4,1)S(1)}, s32[]{:S(2)}) async-start(s8[29360128]{0:T(1024)(128)(4,1)} %bitcast.1), calls=%async_computation.6 | async-start | bytes 8388608
  45.9 8.5 %slice-start.5 = ((s8[29360128]{0:T(1024)(128)(4,1)}), s8[4194304]{0:T(1024)(128)(4,1)S(1)}, s32[]{:S(2)}) async-start(s8[29360128]{0:T(1024)(128)(4,1)} %bitcast.1), calls=%async_computation.7 | async-start | bytes 8388608
  45.9 8.5 %slice-start.6 = ((s8[29360128]{0:T(1024)(128)(4,1)}), s8[4194304]{0:T(1024)(128)(4,1)S(1)}, s32[]{:S(2)}) async-start(s8[29360128]{0:T(1024)(128)(4,1)} %bitcast.1), calls=%async_computation.8 | async-start | bytes 8388608
  46.0 5.8 %collective-permute-start.8 = (bf16[144,128]{1,0:T(8,128)(2,1)S(1)}, bf16[144,128]{1,0:T(8,128)(2,1)S(1)}, u32[]{:S(2)}, u32[]{:S(2)}) collective-permute-start(bf16[144,128]{1,0:T(8,128)(2,1)S(1)} %gated.1.own), channel_id=1, source_target_pairs={{0,12},{1,13},{2,14},{3,15},{4,8},{5,9},{6,10},{7,11},{8,4},{9,5},... | collective-permute-start | bytes 110600 | tf_op jit(solution)/shard_map/ppermute | solution.py:604
  48.3 4.9 %collective-permute-start.7 = (bf16[144,128]{1,0:T(8,128)(2,1)S(1)}, bf16[144,128]{1,0:T(8,128)(2,1)S(1)}, u32[]{:S(2)}, u32[]{:S(2)}) collective-permute-start(bf16[144,128]{1,0:T(8,128)(2,1)S(1)} %gated.1.own), channel_id=1, source_target_pairs={{0,8},{1,9},{2,10},{3,11},{4,12},{5,13},{6,14},{7,15},{8,0},{9,1},... | collective-permute-start | bytes 110600 | tf_op jit(solution)/shard_map/ppermute | solution.py:604
  48.9 4.4 %collective-permute-start.6 = (bf16[144,128]{1,0:T(8,128)(2,1)S(1)}, bf16[144,128]{1,0:T(8,128)(2,1)S(1)}, u32[]{:S(2)}, u32[]{:S(2)}) collective-permute-start(bf16[144,128]{1,0:T(8,128)(2,1)S(1)} %gated.1.own), channel_id=1, source_target_pairs={{0,4},{1,5},{2,6},{3,7},{4,0},{5,1},{6,2},{7,3},{8,12},{9,13},{10,... | collective-permute-start | bytes 110600 | tf_op jit(solution)/shard_map/ppermute | solution.py:604
  53.3 5.2 %collective-permute-start.9 = (bf16[4,144,128]{2,1,0:T(8,128)(2,1)S(1)}, bf16[4,144,128]{2,1,0:T(8,128)(2,1)S(1)}, u32[]{:S(2)}, u32[]{:S(2)}) collective-permute-start(bf16[4,144,128]{2,1,0:T(8,128)(2,1)S(1)} %gather.1.hidden), channel_id=1, source_target_pairs={{0,2},{1,3},{2,0},{3,1},{4,6},{5,7},{6,4},{7,5},{8,10},{9,11},{10,... | collective-permute-start | bytes 442376 | tf_op jit(solution)/shard_map/ppermute | solution.py:606

commit v4 on v3

--- a/solution.py
+++ b/solution.py
@@ -144,7 +144,15 @@
     return high, mid, low
 
 
-def one_block(kernel, outs, args, spaces, name, scratch=(), flops=0, grant=3 << 20):
+def three_rows(line):
+    rows = row_iota((8, HS))
+    tail = jnp.zeros((8, HS), jnp.float32)
+    for at, part in enumerate(split_three(line)):
+        tail = jnp.where(rows == at, part.astype(jnp.float32), tail)
+    return tail.astype(jnp.bfloat16)
+
+
+def one_block(kernel, outs, args, spaces, scratch=(), flops=0, grant=3 << 20):
     return pl.pallas_call(
         kernel,
         out_shape=[jax.ShapeDtypeStruct(shape, dtype) for shape, dtype in outs],
@@ -153,7 +161,6 @@
         scratch_shapes=list(scratch),
         cost_estimate=pl.CostEstimate(flops=flops, transcendentals=0, bytes_accessed=1 << 20),
         compiler_params=pltpu.CompilerParams(vmem_limit_bytes=grant),
-        name=name,
     )(*args)
 
 
@@ -163,9 +170,9 @@
         pltpu.make_async_copy(source, place, sems.at[i])
         for i, (source, place) in enumerate(zip(sources, places))
     ]
-    for copy in copies:
+    for copy in (copies[6], copies[2], *copies[3:6], copies[0], copies[1], copies[7]):
         copy.start()
-    for copy in copies:
+    for copy in copies[2:6]:
         copy.wait()
     ids, scores_in, query, key_new, value_new, stream, keys, values = places
     q_rows, s_rows, own_k, own_v, s_acc = work
@@ -180,6 +187,10 @@
         here = slice(g * group, (g + 1) * group)
         own_k[here, :] = jnp.broadcast_to(key_new[0:1, cut].astype(jnp.float32), (group, HS))
         own_v[here, :] = jnp.broadcast_to(value_new[0:1, cut].astype(jnp.float32), (group, HS))
+    copies[6].wait()
+    for g in range(KVH):
+        cut = slice(g * HS, (g + 1) * HS)
+        here = slice(g * group, (g + 1) * group)
         s_acc[here, :] = lax.dot_general(
             q_rows[here, :].astype(jnp.bfloat16),
             keys[0, :, cut],
@@ -197,6 +208,8 @@
     p_cache = e_cache / total
     p_own = (e_own / total).astype(jnp.bfloat16).astype(jnp.float32)
     s_acc[...] = p_cache
+    for copy in (copies[0], copies[1], copies[7]):
+        copy.wait()
     for g in range(KVH):
         cut = slice(g * HS, (g + 1) * HS)
         here = slice(g * group, (g + 1) * group)
@@ -224,7 +237,7 @@
         out[block, NH + per : rows, :] = tail
 
 
-def project_kernel(weight, here, there, gain, out, resid_out, slot_out, pick_out, rows32, lhs, acc, *, slots):
+def project_kernel(weight, here, there, gain, out, resid_out, place_out, pick_out, rows32, lhs, acc, scaled, *, slots):
     batch, width = acc.shape
     chips, rows = here.shape[:2]
     place = lax.axis_index("gx")
@@ -243,15 +256,11 @@
         resid = stream + acc[:, cut].astype(jnp.bfloat16).astype(jnp.float32)
         resid_out[:, cut] = resid
         power = power + jnp.sum(resid * resid, axis=-1, keepdims=True)
-        scaled = resid * gain[pl.ds(place * per + q, 1), :]
-        out[:, cut] = scaled.astype(jnp.bfloat16)
+        scaled[:, cut] = (resid * gain[pl.ds(place * per + q, 1), :]).astype(jnp.bfloat16)
     lanes = lane_iota((batch, HS))
-    high, mid, low = split_three(jnp.broadcast_to(power, (batch, HS)))
-    zero = jnp.zeros((batch, HS), jnp.float32)
-    packed = jnp.where(lanes == 0, high.astype(jnp.float32), zero)
-    packed = jnp.where(lanes == 1, mid.astype(jnp.float32), packed)
-    packed = jnp.where(lanes == 2, low.astype(jnp.float32), packed)
-    out[:, width : width + HS] = packed.astype(jnp.bfloat16)
+    eye = lanes == row_iota((batch, HS))
+    out[RESIDENT * 16 :, :] = jnp.zeros((8, width), jnp.bfloat16)
+    out[RESIDENT * 16 :, :HS] = three_rows(jnp.sum(jnp.where(eye, power, 0.0), axis=0, keepdims=True))
     tri = (lane_iota((batch, batch)) < row_iota((batch, batch))).astype(jnp.bfloat16)
     onehot = jnp.zeros((batch, HS), jnp.float32)
     picked = jnp.zeros((batch, HS), jnp.float32)
@@ -266,7 +275,12 @@
             onehot = jnp.where(hit, 1.0, onehot)
             if turn == 0:
                 picked = jnp.where(hit, w, picked)
-    slot_out[...] = onehot
+    hot = onehot.astype(jnp.bfloat16)
+    over = (((0,), (0,)), ((), ()))
+    spread = lax.dot_general(hot[:, : RESIDENT * 16], scaled[...], over, preferred_element_type=jnp.float32)
+    out[: RESIDENT * 16, :] = spread.astype(jnp.bfloat16)
+    hot_rows = hot[:, 32 : 32 + place_out.shape[0]]
+    place_out[...] = lax.dot_general(hot_rows, eye.astype(jnp.bfloat16), over, preferred_element_type=jnp.float32)
     pick_out[...] = picked
 
 
@@ -328,40 +342,26 @@
     stacked(work, merged(*gates), merged(*ups), RESIDENT * slots)
 
 
-def far_kernel(mine, other, onehot, gate, up, out, lhs_out, place_out, tail_out, ring, sems, work, *, slots):
-    batch = mine.shape[0]
+def far_kernel(mine, other, gate, up, out, lhs_out, tail_out, ring, sems, work, *, slots):
     place = lax.axis_index("gx")
     side = place // 2 % 2
     blocks = UpBlocks(up, ring, sems, 1 - side)
     lines = 2 * RESIDENT * slots
-    width = mine.shape[1] - HS
-    first = place % 2 == 0
-    own = mine[:, :width].astype(jnp.float32)
-    far = other[:, :width].astype(jnp.float32)
-    left = jnp.where(first, own, far).astype(jnp.bfloat16)
-    right = jnp.where(first, far, own).astype(jnp.bfloat16)
-    hot = onehot[...].astype(jnp.bfloat16)
-    over = (((0,), (0,)), ((), ()))
-    for at, piece in ((0, left), (width, right)):
-        spread = lax.dot_general(hot[:, : RESIDENT * 16], piece, over, preferred_element_type=jnp.float32)
+    width = mine.shape[1]
+
+    def join(fixed):
         for expert in range(RESIDENT):
-            lhs_out[expert, :, at : at + width] = spread[expert * 16 : (expert + 1) * 16].astype(jnp.bfloat16)
-    power = mine[:, width:].astype(jnp.float32) + other[:, width:].astype(jnp.float32)
-    power = jnp.sum(power, axis=-1, keepdims=True)
-    eye = lane_iota((batch, HS)) == row_iota((batch, HS))
-    line = jnp.sum(jnp.where(eye, power, 0.0), axis=0, keepdims=True)
-    high, mid, low = split_three(line)
-    rows = row_iota((8, HS))
-    tail = jnp.where(rows == 0, high.astype(jnp.float32), 0.0)
-    tail = jnp.where(rows == 1, mid.astype(jnp.float32), tail)
-    tail = jnp.where(rows == 2, low.astype(jnp.float32), tail)
-    tail_out[...] = tail
-    hot_rows = hot[:, 32 : 32 + place_out.shape[0]]
-    place_out[...] = lax.dot_general(hot_rows, eye.astype(jnp.bfloat16), over, preferred_element_type=jnp.float32)
+            for at, source in ((fixed, mine), (1 - fixed, other)):
+                lhs_out[expert, :, at * width : (at + 1) * width] = source[expert * 16 : (expert + 1) * 16, :]
+
+    both_sides(place % 2, join)
+    power = mine[RESIDENT * 16 :, :HS].astype(jnp.float32) + other[RESIDENT * 16 :, :HS].astype(jnp.float32)
+    tail = three_rows(jnp.sum(power, axis=0, keepdims=True))
+    tail_out[...] = tail.astype(jnp.float32)
 
     def run(fixed):
         for z in range(out.shape[0]):
-            out[z, out.shape[1] - 8 :, :] = tail.astype(jnp.bfloat16)
+            out[z, out.shape[1] - 8 :, :] = tail
             side_sums(blocks, lhs_out, gate, z, fixed, slots, work)
             for q in range(blocks.narrow // HS):
                 value = work[:, q * HS : (q + 1) * HS]
@@ -457,7 +457,6 @@
         result = term if result is None else result + term
     own = resid[...]
     none = jnp.zeros_like(own)
-    width = own.shape[1]
     result = result + jnp.concatenate(
         [jnp.where(half == 0, own, none), jnp.where(half == 0, none, own)], axis=1
     )
@@ -528,7 +527,6 @@
         [((MSPLIT, rows, HS), bf16)],
         [lengths] + [pltpu.with_memory_space_constraint(value, pltpu.HBM) for value in loaded],
         [pltpu.SMEM] + [pltpu.HBM] * len(loaded),
-        "attend",
         scratch=[(pltpu.SMEM if i < 2 else pltpu.VMEM)(value.shape, value.dtype) for i, value in enumerate(loaded)]
         + [pltpu.SemaphoreType.DMA((len(loaded),))]
         + [
@@ -542,22 +540,22 @@
     )
     chip_rows = exchange(sent, chips)
     other_rows = lax.ppermute(chip_rows, "gx", swap)
-    mine, resid, onehot, picked = one_block(
+    held = -(-RESIDENT * slots // 8) * 8
+    mine, resid, place, picked = one_block(
         functools.partial(project_kernel, slots=slots),
-        [((batch, own_width + HS), bf16), ((batch, own_width), f32), ((batch, HS), f32), ((batch, HS), f32)],
+        [((RESIDENT * 16 + 8, own_width), bf16), ((batch, own_width), f32), ((held, HS), f32), ((batch, HS), f32)],
         (near(out_weight), chip_rows, other_rows, norm_gain.reshape(width // HS, HS)),
         [V, V, V, V],
-        "project",
         scratch=[
             pltpu.VMEM((batch * rows, HS), f32),
             pltpu.VMEM((batch, width), bf16),
             pltpu.VMEM((batch, own_width), f32),
+            pltpu.VMEM((batch, own_width), bf16),
         ],
     )
     other = lax.ppermute(mine, "gx", swap)
     narrow = hidden_cols // MSPLIT
     per = narrow // HS
-    held = -(-RESIDENT * slots // 8) * 8
     chunk = (per * lines + 8, HS)
     flat = (-(-per * RESIDENT * slots // 8) * 8, HS)
     up_hbm = pltpu.with_memory_space_constraint(up_weight, pltpu.HBM)
@@ -569,12 +567,11 @@
             pltpu.VMEM((lines, narrow), f32),
         ]
 
-    far, lhs, place, tail = one_block(
+    far, lhs, tail = one_block(
         functools.partial(far_kernel, slots=slots),
-        [((4,) + chunk, bf16), ((RESIDENT, 16, block_width), bf16), ((held, HS), f32), ((8, HS), f32)],
-        (near(mine), near(other), near(onehot), near(gate_weight), up_hbm),
-        [V, V, V, V, pltpu.HBM],
-        "far",
+        [((4,) + chunk, bf16), ((RESIDENT, 16, block_width), bf16), ((8, HS), f32)],
+        (near(mine), near(other), near(gate_weight), up_hbm),
+        [V, V, V, pltpu.HBM],
         scratch=side_scratch(6),
         grant=7 << 20,
     )
@@ -584,25 +581,27 @@
         [((4,) + chunk, f32)],
         (lhs, tail, near(gate_weight), up_hbm),
         [V, V, V, pltpu.HBM],
-        "near",
         scratch=side_scratch(6),
         grant=7 << 20,
     )
     keep, *sends = one_block(
-        pair_kernel, [(chunk, f32)] + [(chunk, bf16)] * 3, (near_sums, crossed), [V, V], "pair", flops=HINT // 5
-    )
-    got = [lax.ppermute(sends[d - 1], "gx", [(i, i ^ 4 * d) for i in range(members)]) for d in (1, 2, 3)]
+        pair_kernel, [(chunk, f32)] + [(chunk, bf16)] * 3, (near_sums, crossed), [V, V], flops=HINT // 5
+    )
+    got = []
+    for d in (1, 2, 3):
+        got.append(lax.ppermute(sends[d - 1], "gx", [(i, i ^ 4 * d) for i in range(members)]))
     (hidden,) = one_block(
         functools.partial(gated_kernel, slots=slots, width=width),
         [(flat, bf16)],
         (keep, *got, place),
         [V] * 5,
-        "gated",
         scratch=[pltpu.VMEM(chunk, f32), pltpu.VMEM(flat, f32)],
         flops=HINT // 5,
     )
-    parts = [lax.ppermute(hidden, "gx", [(i, i ^ 4 * d) for i in range(members)]) for d in (1, 2, 3)]
-    (near_hidden,) = one_block(gather_kernel, [((4,) + flat, bf16)], (hidden, *parts), [V] * 4, "gather", flops=HG)
+    parts = []
+    for d in (1, 2, 3):
+        parts.append(lax.ppermute(hidden, "gx", [(i, i ^ 4 * d) for i in range(members)]))
+    (near_hidden,) = one_block(gather_kernel, [((4,) + flat, bf16)], (hidden, *parts), [V] * 4, flops=HG)
     far_hidden = lax.ppermute(near_hidden, "gx", [(i, i ^ 2) for i in range(members)])
     side_rows = [pltpu.VMEM((4,) + flat, f32), pltpu.VMEM((4, RESIDENT, 16, narrow), bf16)]
     sums = (RESIDENT * 16, block_width)
@@ -611,7 +610,6 @@
         [(sums, f32)],
         (near_hidden, near(down_weight)),
         [V, V],
-        "down_near",
         scratch=side_rows,
     )
     (partial_out,) = one_block(
@@ -619,11 +617,10 @@
         [((members, block_width // HS, HS), bf16)],
         (far_hidden, near(down_weight), near_acc, picked, resid),
         [V] * 5,
-        "down_far",
         scratch=[pltpu.VMEM((members * block_width // HS, HS), f32)] + side_rows + [pltpu.VMEM(sums, f32)],
     )
     last = exchange(partial_out, None)
-    (out,) = one_block(finish_kernel, [((1, width), bf16)], (last,), [V], "finish")
+    (out,) = one_block(finish_kernel, [((1, width), bf16)], (last,), [V])
     return out
 
 

time: 71.7 us -> 71.8 us (level)
  no operation moved by 1% of the time
where the time goes in v4:
time: 71.8 us; the launch traced here: 71.6 us
  blocking collectives  25 us (35%)
  Pallas kernels  22 us (31%)
  waiting for transfers between devices  12.6 us (18%)
  starting transfers between devices  11.1 us (15%)
  between operations  0.79 us (1%)
    all_to_all x2, blocking collectives, exchange(): lax.all_to_all(value, 'gx', split_axis=0, concat_axis=0, tiled=True, axis...  25 us
    pallas_call x10, Pallas kernels, one_block(): pl.pallas_call(kernel, out_shape=[jax.ShapeDtypeStruct(shape, dtype) for...  22 us
    ppermute x3, starting transfers between devices, fast_on_device(): lax.ppermute(hidden, 'gx', [(i, i ^ 4 * d) for i in range(members)])  4.45 us
    ppermute x3, starting transfers between devices, fast_on_device(): lax.ppermute(sends[d - 1], 'gx', [(i, i ^ 4 * d) for i in range(members)])  4.45 us
    ppermute x3, waiting for transfers between devices, fast_on_device(): lax.ppermute(sends[d - 1], 'gx', [(i, i ^ 4 * d) for i in range(members)])  4.01 us
    ppermute x3, waiting for transfers between devices, fast_on_device(): lax.ppermute(hidden, 'gx', [(i, i ^ 4 * d) for i in range(members)])  2.77 us
    ppermute x1, waiting for transfers between devices, fast_on_device(): lax.ppermute(near_hidden, 'gx', [(i, i ^ 2) for i in range(members)])  1.92 us
    ppermute x1, waiting for transfers between devices, fast_on_device(): crossed = lax.ppermute(far, 'gx', [(i, i ^ 2) for i in range(members)])  1.44 us
  transfers between devices with their start and end apart: 10, of which 8 were waited for; matrix products, arithmetic and copies ran while one was open for 0% of the time, Pallas kernels for 12%

profile of v4, /device:TPU:0, one launch (start us, length us, event | category | flops | bytes accessed | tf_op | source)
XLA Modules:
  0.0 71.6 jit_solution(611208731175335884)
XLA Ops:
  0.7 0.0 copy-start.1
  0.7 0.0 copy-start.2
  0.7 0.0 copy-start
  0.7 1.8 %shard_map.136 = bf16[8,80,128]{2,1,0:T(8,128)(2,1)S(1)} custom-call(s32[1]{0:T(128)S(6)} %copy.15.refs_0_, s32[1,2]{1,0:T(1,128)} %refs_1_.1, f32[1,2]{1,0:T(1,128)} %refs_2_.1, bf16[1,8192]{1,0:T(2,128)(2,1)} %refs_3_.1, bf16[1,1024]{1,0:T(2,128)(2,1)} %refs_4_.1, bf16[1,1024]{1,0:T(2,128)(2,1)} %refs_5_.1, bf16[1,8192]{1,0:T(2,128)(2,1)} %refs_6_.1, ...), custom_call_target="tpu_custom_call" | custom-call | flops 99999997952 | bytes 1048576 | tf_op jit(solution)/shard_map/pallas_call | solution.py:156
  2.5 14.9 %all_to_all.10.here = bf16[8,80,128]{2,1,0:T(8,128)(2,1)S(1)} all-to-all(bf16[8,80,128]{2,1,0:T(8,128)(2,1)S(1)} %shard_map.136), channel_id=1, replica_groups={{0,2,4,6,8,10,12,14},{1,3,5,7,9,11,13,15},{16,18,20,22,24,26,28,30},{17..., dimensions={0} | all-to-all | bytes 327680 | tf_op jit(solution)/shard_map/all_to_all | solution.py:520
  17.4 0.0 collective-permute-start
  17.4 1.4 %collective-permute-done.there = bf16[8,80,128]{2,1,0:T(8,128)(2,1)S(1)} collective-permute-done((bf16[8,80,128]{2,1,0:T(8,128)(2,1)S(1)}, bf16[8,80,128]{2,1,0:T(8,128)(2,1)S(1)}, u32[]{:S(2)}, u32[]{:S(2)}) %collective-permute-start) | collective-permute-done | bytes 163872 | tf_op jit(solution)/shard_map/ppermute | solution.py:542
  18.8 0.0 copy-done.1
  18.8 0.0 copy-done.2
  18.8 1.5 %shard_map.137 = (bf16[40,512]{1,0:T(8,128)(2,1)S(1)}, f32[16,512]{1,0:T(8,128)S(1)}, f32[24,128]{1,0:T(8,128)S(1)}, f32[16,128]{1,0:T(8,128)S(1)}) custom-call(bf16[8192,512]{1,0:T(8,128)(2,1)S(1)} %copy-done.1, bf16[8,80,128]{2,1,0:T(8,128)(2,1)S(1)} %all_to_all.10.here, bf16[8,80,128]{2,1,0:T(8,128)(2,1)S(1)} %collective-permute-done.there, ...), custom_call_target="tpu_custom_call" | custom-call | bytes 1048576 | tf_op jit(solution)/shard_map/pallas_call | solution.py:156
  20.3 0.2 collective-permute-start.1
  20.5 1.1 %collective-permute-done.1.other = bf16[40,512]{1,0:T(8,128)(2,1)S(1)} collective-permute-done((bf16[40,512]{1,0:T(8,128)(2,1)S(1)}, bf16[40,512]{1,0:T(8,128)(2,1)S(1)}, u32[]{:S(2)}, u32[]{:S(2)}) %collective-permute-start.1) | collective-permute-done | bytes 40992 | tf_op jit(solution)/shard_map/ppermute | solution.py:556
  21.5 0.0 copy-done
  21.5 6.7 %shard_map.138 = (bf16[4,288,128]{2,1,0:T(8,128)(2,1)S(1)}, bf16[2,16,1024]{2,1,0:T(8,128)(2,1)S(1)}, f32[8,128]{1,0:T(8,128)S(1)}) custom-call(bf16[40,512]{1,0:T(8,128)(2,1)S(1)} %get-tuple-element.16.mine, bf16[40,512]{1,0:T(8,128)(2,1)S(1)} %collective-permute-done.1.other, bf16[2,1024,7168]{2,1,0:T(8,128)(2,1)S(1)} %copy-done, bf16[2,1024,7168]{2,1,0:T(8,128)(2,1)} %up.3), custom_call_target="tpu_custom_call" | custom-call | bytes 1048576 | tf_op jit(solution)/shard_map/pallas_call | solution.py:156
  28.3 1.0 %collective-permute-start.2 = (bf16[4,288,128]{2,1,0:T(8,128)(2,1)S(1)}, bf16[4,288,128]{2,1,0:T(8,128)(2,1)S(1)}, u32[]{:S(2)}, u32[]{:S(2)}) collective-permute-start(bf16[4,288,128]{2,1,0:T(8,128)(2,1)S(1)} %get-tuple-element.19), channel_id=1, source_target_pairs={{0,2},{1,3},{2,0},{3,1},{4,6},{5,7},{6,4},{7,5},{8,10},{9,11},{10,... | collective-permute-start | bytes 884744 | tf_op jit(solution)/shard_map/ppermute | solution.py:578
  29.2 6.7 %shard_map.139.near_sums = f32[4,288,128]{2,1,0:T(8,128)S(1)} custom-call(bf16[2,16,1024]{2,1,0:T(8,128)(2,1)S(1)} %get-tuple-element.17.lhs, f32[8,128]{1,0:T(8,128)S(1)} %get-tuple-element.18.tail, bf16[2,1024,7168]{2,1,0:T(8,128)(2,1)S(1)} %copy-done, bf16[2,1024,7168]{2,1,0:T(8,128)(2,1)} %up.3), custom_call_target="tpu_custom_call" | custom-call | bytes 1048576 | tf_op jit(solution)/shard_map/pallas_call | solution.py:156
  36.0 1.4 %collective-permute-done.2.got = bf16[4,288,128]{2,1,0:T(8,128)(2,1)S(1)} collective-permute-done((bf16[4,288,128]{2,1,0:T(8,128)(2,1)S(1)}, bf16[4,288,128]{2,1,0:T(8,128)(2,1)S(1)}, u32[]{:S(2)}, u32[]{:S(2)}) %collective-permute-start.2) | collective-permute-done | bytes 294944 | tf_op jit(solution)/shard_map/ppermute | solution.py:578
  37.4 0.0 slice-start
  37.4 0.0 slice-start.2
  37.4 0.0 slice-start.3
  37.4 0.1 shard_map.140
  37.5 0.3 collective-permute-start.3
  37.8 1.0 %collective-permute-start.4 = (bf16[288,128]{1,0:T(8,128)(2,1)S(1)}, bf16[288,128]{1,0:T(8,128)(2,1)S(1)}, u32[]{:S(2)}, u32[]{:S(2)}) collective-permute-start(bf16[288,128]{1,0:T(8,128)(2,1)S(1)} %get-tuple-element.22), channel_id=1, source_target_pairs={{0,8},{1,9},{2,10},{3,11},{4,12},{5,13},{6,14},{7,15},{8,0},{9,1},... | collective-permute-start | bytes 221192 | tf_op jit(solution)/shard_map/ppermute | solution.py:592
  38.8 3.2 %collective-permute-start.5 = (bf16[288,128]{1,0:T(8,128)(2,1)S(1)}, bf16[288,128]{1,0:T(8,128)(2,1)S(1)}, u32[]{:S(2)}, u32[]{:S(2)}) collective-permute-start(bf16[288,128]{1,0:T(8,128)(2,1)S(1)} %get-tuple-element.23), channel_id=1, source_target_pairs={{0,12},{1,13},{2,14},{3,15},{4,8},{5,9},{6,10},{7,11},{8,4},{9,5},... | collective-permute-start | bytes 221192 | tf_op jit(solution)/shard_map/ppermute | solution.py:592
  41.9 0.1 collective-permute-done.3.first
  42.0 3.9 %collective-permute-done.4.second = bf16[288,128]{1,0:T(8,128)(2,1)S(1)} collective-permute-done((bf16[288,128]{1,0:T(8,128)(2,1)S(1)}, bf16[288,128]{1,0:T(8,128)(2,1)S(1)}, u32[]{:S(2)}, u32[]{:S(2)}) %collective-permute-start.4) | collective-permute-done | bytes 73760 | tf_op jit(solution)/shard_map/ppermute | solution.py:592
  45.9 0.0 collective-permute-done.5.third
  46.0 0.0 slice-start.4
  46.0 0.1 shard_map.141.own
  46.1 2.3 %collective-permute-start.8 = (bf16[144,128]{1,0:T(8,128)(2,1)S(1)}, bf16[144,128]{1,0:T(8,128)(2,1)S(1)}, u32[]{:S(2)}, u32[]{:S(2)}) collective-permute-start(bf16[144,128]{1,0:T(8,128)(2,1)S(1)} %shard_map.141.own), channel_id=1, source_target_pairs={{0,12},{1,13},{2,14},{3,15},{4,8},{5,9},{6,10},{7,11},{8,4},{9,5},... | collective-permute-start | bytes 110600 | tf_op jit(solution)/shard_map/ppermute | solution.py:603
  48.4 0.6 collective-permute-start.7
  49.0 1.6 %collective-permute-start.6 = (bf16[144,128]{1,0:T(8,128)(2,1)S(1)}, bf16[144,128]{1,0:T(8,128)(2,1)S(1)}, u32[]{:S(2)}, u32[]{:S(2)}) collective-permute-start(bf16[144,128]{1,0:T(8,128)(2,1)S(1)} %shard_map.141.own), channel_id=1, source_target_pairs={{0,4},{1,5},{2,6},{3,7},{4,0},{5,1},{6,2},{7,3},{8,12},{9,13},{10,... | collective-permute-start | bytes 110600 | tf_op jit(solution)/shard_map/ppermute | solution.py:603
  50.6 1.4 %collective-permute-done.8.third = bf16[144,128]{1,0:T(8,128)(2,1)S(1)} collective-permute-done((bf16[144,128]{1,0:T(8,128)(2,1)S(1)}, bf16[144,128]{1,0:T(8,128)(2,1)S(1)}, u32[]{:S(2)}, u32[]{:S(2)}) %collective-permute-start.8) | collective-permute-done | bytes 36896 | tf_op jit(solution)/shard_map/ppermute | solution.py:603
  51.9 1.4 %collective-permute-done.7.second = bf16[144,128]{1,0:T(8,128)(2,1)S(1)} collective-permute-done((bf16[144,128]{1,0:T(8,128)(2,1)S(1)}, bf16[144,128]{1,0:T(8,128)(2,1)S(1)}, u32[]{:S(2)}, u32[]{:S(2)}) %collective-permute-start.7) | collective-permute-done | bytes 36896 | tf_op jit(solution)/shard_map/ppermute | solution.py:603
  53.3 0.0 collective-permute-done.6.first
  53.4 1.1 %collective-permute-start.9 = (bf16[4,144,128]{2,1,0:T(8,128)(2,1)S(1)}, bf16[4,144,128]{2,1,0:T(8,128)(2,1)S(1)}, u32[]{:S(2)}, u32[]{:S(2)}) collective-permute-start(bf16[4,144,128]{2,1,0:T(8,128)(2,1)S(1)} %shard_map.142.hidden), channel_id=1, source_target_pairs={{0,2},{1,3},{2,0},{3,1},{4,6},{5,7},{6,4},{7,5},{8,10},{9,11},{10,... | collective-permute-start | bytes 442376 | tf_op jit(solution)/shard_map/ppermute | solution.py:605
  54.4 0.0 slice-done
  54.4 0.0 slice-done.1
  54.4 0.0 slice-done.2
  54.4 0.0 slice-done.3
  54.4 0.0 slice-done.4
  54.4 0.0 slice-done.5
  54.4 0.0 slice-done.6
  54.5 2.2 %shard_map.143.near_acc = f32[32,1024]{1,0:T(8,128)S(1)} custom-call(bf16[4,144,128]{2,1,0:T(8,128)(2,1)S(1)} %shard_map.142.hidden, bf16[2,7168,1024]{2,1,0:T(8,128)(2,1)S(1)} %bitcast.2), custom_call_target="tpu_custom_call" | custom-call | bytes 1048576 | tf_op jit(solution)/shard_map/pallas_call | solution.py:156
  56.6 1.9 %collective-permute-done.9.hidden = bf16[4,144,128]{2,1,0:T(8,128)(2,1)S(1)} collective-permute-done((bf16[4,144,128]{2,1,0:T(8,128)(2,1)S(1)}, bf16[4,144,128]{2,1,0:T(8,128)(2,1)S(1)}, u32[]{:S(2)}, u32[]{:S(2)}) %collective-permute-start.9) | collective-permute-done | bytes 147488 | tf_op jit(solution)/shard_map/ppermute | solution.py:605
  58.6 2.3 %shard_map.144 = bf16[16,8,128]{2,1,0:T(8,128)(2,1)S(1)} custom-call(bf16[4,144,128]{2,1,0:T(8,128)(2,1)S(1)} %collective-permute-done.9.hidden, bf16[2,7168,1024]{2,1,0:T(8,128)(2,1)S(1)} %bitcast.2, f32[32,1024]{1,0:T(8,128)S(1)} %shard_map.143.near_acc, f32[16,128]{1,0:T(8,128)S(1)} %get-tuple-element.25.picked, f32[16,512]{1,0:T(8,128)S(1)} %get-tuple-element.26.resid), custom_call_target="tpu_custom_call" | custom-call | bytes 1048576 | tf_op jit(solution)/shard_map/pallas_call | solution.py:156
  60.8 10.1 %all_to_all.11.got = bf16[16,8,128]{2,1,0:T(8,128)(2,1)S(1)} all-to-all(bf16[16,8,128]{2,1,0:T(8,128)(2,1)S(1)} %shard_map.144), channel_id=1, replica_groups=mesh['groups'=2,'gx'=16] {'gx'}, dimensions={0} | all-to-all | bytes 65536 | tf_op jit(solution)/shard_map/all_to_all | solution.py:520
  70.9 0.6 shard_map.145
  (5 shorter events, 0.0 us)
Async XLA Ops:
  0.7 18.1 %copy-start.1 = (bf16[8192,512]{1,0:T(8,128)(2,1)S(1)}, bf16[8192,512]{1,0:T(8,128)(2,1)}, u32[]{:S(2)}) copy-start(bf16[8192,512]{1,0:T(8,128)(2,1)} %weight.1) | copy-start | bytes 25165828
  0.7 18.1 %copy-start.2 = (f32[8192]{0:T(1024)S(1)}, f32[8192]{0:T(1024)}, u32[]{:S(2)}) copy-start(f32[8192]{0:T(1024)} %param.24) | copy-start | bytes 98308
  0.7 20.9 %copy-start = (bf16[2,1024,7168]{2,1,0:T(8,128)(2,1)S(1)}, bf16[2,1024,7168]{2,1,0:T(8,128)(2,1)}, u32[]{:S(2)}) copy-start(bf16[2,1024,7168]{2,1,0:T(8,128)(2,1)} %gate.3) | copy-start | bytes 88080384
  17.4 1.4 %collective-permute-start = (bf16[8,80,128]{2,1,0:T(8,128)(2,1)S(1)}, bf16[8,80,128]{2,1,0:T(8,128)(2,1)S(1)}, u32[]{:S(2)}, u32[]{:S(2)}) collective-permute-start(bf16[8,80,128]{2,1,0:T(8,128)(2,1)S(1)} %all_to_all.10.here), channel_id=1, source_target_pairs={{0,1},{1,0},{2,3},{3,2},{4,5},{5,4},{6,7},{7,6},{8,9},{9,8},{10,11... | collective-permute-start | bytes 491528 | tf_op jit(solution)/shard_map/ppermute | solution.py:542
  20.3 1.3 %collective-permute-start.1 = (bf16[40,512]{1,0:T(8,128)(2,1)S(1)}, bf16[40,512]{1,0:T(8,128)(2,1)S(1)}, u32[]{:S(2)}, u32[]{:S(2)}) collective-permute-start(bf16[40,512]{1,0:T(8,128)(2,1)S(1)} %get-tuple-element.16.mine), channel_id=1, source_target_pairs={{0,1},{1,0},{2,3},{3,2},{4,5},{5,4},{6,7},{7,6},{8,9},{9,8},{10,11... | collective-permute-start | bytes 122888 | tf_op jit(solution)/shard_map/ppermute | solution.py:556
  28.3 9.1 %collective-permute-start.2 = (bf16[4,288,128]{2,1,0:T(8,128)(2,1)S(1)}, bf16[4,288,128]{2,1,0:T(8,128)(2,1)S(1)}, u32[]{:S(2)}, u32[]{:S(2)}) collective-permute-start(bf16[4,288,128]{2,1,0:T(8,128)(2,1)S(1)} %get-tuple-element.19), channel_id=1, source_target_pairs={{0,2},{1,3},{2,0},{3,1},{4,6},{5,7},{6,4},{7,5},{8,10},{9,11},{10,... | collective-permute-start | bytes 884744 | tf_op jit(solution)/shard_map/ppermute | solution.py:578
  37.4 17.0 %slice-start = ((s8[29360128]{0:T(1024)(128)(4,1)}), s8[4194304]{0:T(1024)(128)(4,1)S(1)}, s32[]{:S(2)}) async-start(s8[29360128]{0:T(1024)(128)(4,1)} %bitcast.1), calls=%async_computation.2 | async-start | bytes 8388608
  37.4 17.0 %slice-start.1 = ((s8[29360128]{0:T(1024)(128)(4,1)}), s8[4194304]{0:T(1024)(128)(4,1)S(1)}, s32[]{:S(2)}) async-start(s8[29360128]{0:T(1024)(128)(4,1)} %bitcast.1), calls=%async_computation.3 | async-start | bytes 8388608
  37.4 17.0 %slice-start.2 = ((s8[29360128]{0:T(1024)(128)(4,1)}), s8[4194304]{0:T(1024)(128)(4,1)S(1)}, s32[]{:S(2)}) async-start(s8[29360128]{0:T(1024)(128)(4,1)} %bitcast.1), calls=%async_computation.4 | async-start | bytes 8388608
  37.4 17.0 %slice-start.3 = ((s8[29360128]{0:T(1024)(128)(4,1)}), s8[4194304]{0:T(1024)(128)(4,1)S(1)}, s32[]{:S(2)}) async-start(s8[29360128]{0:T(1024)(128)(4,1)} %bitcast.1), calls=%async_computation.5 | async-start | bytes 8388608
  37.5 4.5 %collective-permute-start.3 = (bf16[288,128]{1,0:T(8,128)(2,1)S(1)}, bf16[288,128]{1,0:T(8,128)(2,1)S(1)}, u32[]{:S(2)}, u32[]{:S(2)}) collective-permute-start(bf16[288,128]{1,0:T(8,128)(2,1)S(1)} %get-tuple-element.21), channel_id=1, source_target_pairs={{0,4},{1,5},{2,6},{3,7},{4,0},{5,1},{6,2},{7,3},{8,12},{9,13},{10,... | collective-permute-start | bytes 221192 | tf_op jit(solution)/shard_map/ppermute | solution.py:592
  37.8 8.2 %collective-permute-start.4 = (bf16[288,128]{1,0:T(8,128)(2,1)S(1)}, bf16[288,128]{1,0:T(8,128)(2,1)S(1)}, u32[]{:S(2)}, u32[]{:S(2)}) collective-permute-start(bf16[288,128]{1,0:T(8,128)(2,1)S(1)} %get-tuple-element.22), channel_id=1, source_target_pairs={{0,8},{1,9},{2,10},{3,11},{4,12},{5,13},{6,14},{7,15},{8,0},{9,1},... | collective-permute-start | bytes 221192 | tf_op jit(solution)/shard_map/ppermute | solution.py:592
  38.8 7.2 %collective-permute-start.5 = (bf16[288,128]{1,0:T(8,128)(2,1)S(1)}, bf16[288,128]{1,0:T(8,128)(2,1)S(1)}, u32[]{:S(2)}, u32[]{:S(2)}) collective-permute-start(bf16[288,128]{1,0:T(8,128)(2,1)S(1)} %get-tuple-element.23), channel_id=1, source_target_pairs={{0,12},{1,13},{2,14},{3,15},{4,8},{5,9},{6,10},{7,11},{8,4},{9,5},... | collective-permute-start | bytes 221192 | tf_op jit(solution)/shard_map/ppermute | solution.py:592
  46.0 8.5 %slice-start.4 = ((s8[29360128]{0:T(1024)(128)(4,1)}), s8[4194304]{0:T(1024)(128)(4,1)S(1)}, s32[]{:S(2)}) async-start(s8[29360128]{0:T(1024)(128)(4,1)} %bitcast.1), calls=%async_computation.6 | async-start | bytes 8388608
  46.0 8.5 %slice-start.5 = ((s8[29360128]{0:T(1024)(128)(4,1)}), s8[4194304]{0:T(1024)(128)(4,1)S(1)}, s32[]{:S(2)}) async-start(s8[29360128]{0:T(1024)(128)(4,1)} %bitcast.1), calls=%async_computation.7 | async-start | bytes 8388608
  46.0 8.5 %slice-start.6 = ((s8[29360128]{0:T(1024)(128)(4,1)}), s8[4194304]{0:T(1024)(128)(4,1)S(1)}, s32[]{:S(2)}) async-start(s8[29360128]{0:T(1024)(128)(4,1)} %bitcast.1), calls=%async_computation.8 | async-start | bytes 8388608
  46.1 5.8 %collective-permute-start.8 = (bf16[144,128]{1,0:T(8,128)(2,1)S(1)}, bf16[144,128]{1,0:T(8,128)(2,1)S(1)}, u32[]{:S(2)}, u32[]{:S(2)}) collective-permute-start(bf16[144,128]{1,0:T(8,128)(2,1)S(1)} %shard_map.141.own), channel_id=1, source_target_pairs={{0,12},{1,13},{2,14},{3,15},{4,8},{5,9},{6,10},{7,11},{8,4},{9,5},... | collective-permute-start | bytes 110600 | tf_op jit(solution)/shard_map/ppermute | solution.py:603
  48.4 4.9 %collective-permute-start.7 = (bf16[144,128]{1,0:T(8,128)(2,1)S(1)}, bf16[144,128]{1,0:T(8,128)(2,1)S(1)}, u32[]{:S(2)}, u32[]{:S(2)}) collective-permute-start(bf16[144,128]{1,0:T(8,128)(2,1)S(1)} %shard_map.141.own), channel_id=1, source_target_pairs={{0,8},{1,9},{2,10},{3,11},{4,12},{5,13},{6,14},{7,15},{8,0},{9,1},... | collective-permute-start | bytes 110600 | tf_op jit(solution)/shard_map/ppermute | solution.py:603
  49.0 4.4 %collective-permute-start.6 = (bf16[144,128]{1,0:T(8,128)(2,1)S(1)}, bf16[144,128]{1,0:T(8,128)(2,1)S(1)}, u32[]{:S(2)}, u32[]{:S(2)}) collective-permute-start(bf16[144,128]{1,0:T(8,128)(2,1)S(1)} %shard_map.141.own), channel_id=1, source_target_pairs={{0,4},{1,5},{2,6},{3,7},{4,0},{5,1},{6,2},{7,3},{8,12},{9,13},{10,... | collective-permute-start | bytes 110600 | tf_op jit(solution)/shard_map/ppermute | solution.py:603
  53.4 5.2 %collective-permute-start.9 = (bf16[4,144,128]{2,1,0:T(8,128)(2,1)S(1)}, bf16[4,144,128]{2,1,0:T(8,128)(2,1)S(1)}, u32[]{:S(2)}, u32[]{:S(2)}) collective-permute-start(bf16[4,144,128]{2,1,0:T(8,128)(2,1)S(1)} %shard_map.142.hidden), channel_id=1, source_target_pairs={{0,2},{1,3},{2,0},{3,1},{4,6},{5,7},{6,4},{7,5},{8,10},{9,11},{10,... | collective-permute-start | bytes 442376 | tf_op jit(solution)/shard_map/ppermute | solution.py:605
